TPU v7x, 256 devices: a whole 4x4x8 slice. The times are simulated.
256 devices in a mesh: dp: 64 (over z, x, core), psr: 4 (over y).
Axes of the slice: x: 4, y: 4, z: 8, core: 2. Of those that a mesh axis runs over, the one named last changes fastest.
Arguments:
- basis: bfloat16 [256, 4, 8, 128, 256], P(('dp', 'psr')), may hold values from -6 to 6
- residual: bfloat16 [256, 4, 8, 128], P(('dp', 'psr')), may hold values from -6 to 6
- sigma: bfloat16 [256, 4, 8, 128], P(('dp', 'psr')), may hold values from 0.5 to 2
- counts: int32 [256, 4, 8], P(('dp', 'psr')), may hold values from 0 to 128
- pulsar: int32 [256, 4, 8], P(('dp', 'psr')), may hold values from 0 to 3
- ecorr: float32 [16], replicated, may hold values from 0.2 to 2
Outputs:
- gram: float32 [16, 256, 256], P('psr', 'dp')
- rhs: float32 [16, 256], P('psr', 'dp')
- totals: float32 [2], replicated
All inputs are finite; a program needn't handle non-finite values.
Results may differ from a plain program's by a relative error of at most 0.0055.
Values may be sent and summed in bfloat16 or wider, within the bound.
No kernel may reach another device: no remote copies, remote signals or barrier semaphores. Data moves between devices by JAX's collectives and lax.ppermute only.
A program may use at most 64 MiB of HBM per device.

v0:
```python
import functools

import jax
import jax.numpy as jnp
from jax import lax
from jax.experimental import pallas as pl
from jax.experimental.pallas import tpu as pltpu
from jax.sharding import Mesh
from jax.sharding import PartitionSpec as P


PG = 4
ORDER = (2, 1, 3, 0)
AXES = ("z", "x", "c", "psr")
BF = jnp.bfloat16
F32 = jnp.float32
HALF = 128
GRANT = 16 * 2**20
DIRECT = (((0,), (0,)), ((), ()))


def split2(e):
    head = e.astype(BF).astype(F32)
    return jnp.concatenate([head, e - head], axis=0).astype(BF)


def joined2(x):
    full = x.astype(F32)
    rows = full.shape[0] // 2
    return full[:rows] + full[rows:]


def row_in(rows, width, items):
    sub = lax.broadcasted_iota(jnp.int32, (rows, width), 0)
    out = jnp.zeros((rows, width), F32)
    for at, item in items:
        out = jnp.where(sub == at, jnp.broadcast_to(item, (rows, width)), out)
    return out


def dot0(a, b):
    return lax.dot_general(a, b, DIRECT, preferred_element_type=F32)


def packed(full, rhs, totals):
    a = full[:HALF, :HALF]
    b = full[:HALF, HALF:]
    d = full[HALF:, HALF:]
    r = lax.broadcasted_iota(jnp.int32, (HALF, HALF), 0)
    c = lax.broadcasted_iota(jnp.int32, (HALF, HALF), 1)
    both = jnp.where(r >= c, a, d)
    diag = jnp.sum(jnp.where(r == c, d, 0.0), axis=0, keepdims=True)
    extras = row_in(
        8, HALF, [(0, diag), (1, rhs[:, :HALF]), (2, rhs[:, HALF:]), (3, totals)]
    )
    return b, both, extras


def prepare(i, g, counts, pulsar, ecorr, sigma, residual, rows_s, wide_s, member_s):
    slots = counts.shape[1]
    lane = lax.broadcasted_iota(jnp.int32, (slots, HALF), 1)
    sub = lax.broadcasted_iota(jnp.int32, (slots, HALF), 0)
    count = jnp.zeros((slots, HALF), jnp.int32)
    member = jnp.zeros((slots, HALF), jnp.int32)
    amp = jnp.zeros((slots, HALF), F32)
    for s in range(slots):
        mine = pulsar[g, s]
        count = jnp.where(sub == s, counts[g, s], count)
        member = jnp.where(sub == s, mine, member)
        amp = jnp.where(sub == s, ecorr[g * PG + mine], amp)
    sig = sigma[g].astype(F32)
    res = residual[g].astype(F32)
    square = sig * sig
    valid = lane < count
    inverse = jnp.where(valid, 1.0 / square, 0.0)
    scaled = inverse * res
    total = jnp.sum(inverse, axis=1, keepdims=True)
    wsum = jnp.sum(scaled, axis=1, keepdims=True)
    jitter = amp * amp
    grown = 1.0 + jitter * total
    coef = jitter / grown
    logs = jnp.sum(jnp.where(valid, jnp.log(square), 0.0), axis=1, keepdims=True)
    rows_s[i, 0] = inverse
    rows_s[i, 1] = res
    wide_s[i, 0] = coef
    wide_s[i, 1] = coef * wsum
    member_s[i] = member
    logdet = logs + jnp.log(grown)[:, :1]
    chi = jnp.sum(scaled * res, axis=1, keepdims=True) - coef[:, :1] * wsum * wsum
    return logdet, chi


def gram_of(at_out, blocks, rows, wide, member, totals, core, acc, racc, keep, send):
    slots = blocks.shape[0]
    acc[...] = jnp.zeros_like(acc)
    racc[...] = jnp.zeros_like(racc)
    inverse_t = jnp.transpose(rows[0])
    res_t = jnp.transpose(rows[1])
    coef, pull = wide[0], wide[1]
    columns = []
    for s in range(slots):
        block = blocks[s]
        weighted = (block.astype(F32) * inverse_t[:, s : s + 1]).astype(BF)
        weighted_f = weighted.astype(F32)
        column = jnp.sum(weighted_f, axis=0, keepdims=True)
        project = jnp.sum(weighted_f * res_t[:, s : s + 1], axis=0, keepdims=True)
        mine = member[s, 0]
        acc[mine] += dot0(block, weighted)
        racc[mine, 0:1, :] += project - pull[s : s + 1, 0:1] * column
        columns.append((s, column))
    cols = row_in(slots, 2 * HALF, columns)
    head = cols.astype(BF).astype(F32)
    rest = cols - head
    left = jnp.concatenate([head, rest, head, rest], axis=0).astype(BF)
    nothing = jnp.zeros((1, HALF), F32)
    for at in range(PG):
        to = (core if at < 2 else 1 - core) * 2 + at % 2
        scale = jnp.where(member == to, coef, 0.0)
        scaled = jnp.concatenate([scale, scale], axis=1) * cols
        high = scaled.astype(BF).astype(F32)
        low = scaled - high
        right = jnp.concatenate([high, high, low, low], axis=0).astype(BF)
        full = acc[to] - dot0(left, right)
        b, both, extras = packed(
            full, racc[to, 0:1, :], totals if at % 2 == 0 else nothing
        )
        if at < 2:
            keep[at_out, at, 0:HALF, :] = b
            keep[at_out, at, HALF : 2 * HALF, :] = both
            keep[at_out, at, 2 * HALF :, :] = extras
        else:
            send[at_out, at - 2, 0:HALF, :] = b.astype(BF)
            send[at_out, at - 2, HALF : 2 * HALF, :] = both.astype(BF)
            send[at_out, at - 2, 2 * HALF :, :] = split2(extras)


def first_kernel(
    counts_h, pulsar_h, ecorr_h, sigma_h, residual_h, basis,
    keep, send, later, rows_o, wide_o, member_o, totals_o,
    counts, pulsar, ecorr, sigma, residual, small_sems, buf, sems, acc, racc, rows_s, wide_s, member_s,
):
    y = lax.axis_index("psr")
    core = lax.axis_index("c")
    small = [
        pltpu.make_async_copy(source, target, small_sems.at[k])
        for k, (source, target) in enumerate(
            (
                (counts_h, counts),
                (pulsar_h, pulsar),
                (ecorr_h, ecorr),
                (sigma_h, sigma),
                (residual_h, residual),
            )
        )
    ]
    for copy in small:
        copy.start()
    copies = []
    for k, i in enumerate(ORDER):
        target = buf if k == 0 else later.at[k - 1]
        copies.append(pltpu.make_async_copy(basis.at[y ^ i], target, sems.at[k]))
        copies[-1].start()
    for copy in small:
        copy.wait()
    logdet, chi = 0.0, 0.0
    for k, i in enumerate(ORDER):
        places = (rows_s, wide_s, member_s, 0) if k == 0 else (rows_o, wide_o, member_o, k - 1)
        part = prepare(places[3], y ^ i, counts, pulsar, ecorr, sigma, residual, *places[:3])
        logdet, chi = logdet + part[0], chi + part[1]
    lane1 = lax.broadcasted_iota(jnp.int32, (1, HALF), 1)
    totals = jnp.where(
        lane1 == 0,
        jnp.sum(logdet, axis=0, keepdims=True),
        jnp.where(lane1 == 1, jnp.sum(chi, axis=0, keepdims=True), 0.0),
    )
    totals_o[...] = jnp.broadcast_to(totals, totals_o.shape)
    copies[0].wait()
    gram_of(0, buf, rows_s[0], wide_s[0], member_s[0], totals, core, acc, racc, keep, send)
    for copy in copies[1:]:
        copy.wait()


def later_kernel(which, later, rows, wide, member, totals, after, keep, send, acc, racc):
    core = lax.axis_index("c")
    for k, i in enumerate(which):
        gram_of(
            k, later.at[i], rows[i], wide[i], member[i], totals[0:1], core, acc, racc, keep, send
        )


def packs(n):
    return [((n, 2, 2 * HALF + 8, HALF), F32), ((n, 2, 2 * HALF + 16, HALF), BF)]


def accumulators(width):
    return [pltpu.VMEM((PG, width, width), F32), pltpu.VMEM((PG, 8, width), F32)]


def first_terms(basis, residual, sigma, counts, pulsar, ecorr):
    groups, slots, rows, width = basis.shape
    operands = (counts, pulsar, ecorr, sigma, residual, basis)
    return call(
        first_kernel,
        packs(1)
        + [
            ((groups - 1, slots, rows, width), BF),
            ((groups - 1, 2, slots, rows), F32),
            ((groups - 1, 2, slots, rows), F32),
            ((groups - 1, slots, rows), jnp.int32),
            ((8, HALF), F32),
        ],
        [
            pltpu.SMEM((groups, slots), jnp.int32),
            pltpu.SMEM((groups, slots), jnp.int32),
            pltpu.SMEM(ecorr.shape, F32),
            pltpu.VMEM((groups, slots, rows), BF),
            pltpu.VMEM((groups, slots, rows), BF),
            pltpu.SemaphoreType.DMA((5,)),
            pltpu.VMEM((slots, rows, width), BF),
            pltpu.SemaphoreType.DMA((groups,)),
            *accumulators(width),
            pltpu.VMEM((1, 2, slots, rows), F32),
            pltpu.VMEM((1, 2, slots, rows), F32),
            pltpu.VMEM((1, slots, rows), jnp.int32),
        ],
        [pltpu.with_memory_space_constraint(a, pltpu.HBM) for a in operands],
        in_specs=[pl.BlockSpec(memory_space=pltpu.HBM)] * 6,
    )


def later_terms(which, shared, after):
    vmem = pl.BlockSpec(memory_space=pltpu.VMEM)
    return call(
        functools.partial(later_kernel, which),
        packs(len(which)),
        accumulators(shared[0].shape[-1]),
        (*shared, after),
        in_specs=[vmem] * len(shared) + [pl.BlockSpec(memory_space=pl.ANY)],
        flops=len(which) * 10**9,
    )


def cores_kernel(at, keep, got, out):
    for j in range(2):
        body = keep[at, j, : 2 * HALF] + got[at, j, : 2 * HALF].astype(F32)
        out[j, : 2 * HALF] = body.astype(BF)
        out[j, 2 * HALF :] = split2(keep[at, j, 2 * HALF :] + joined2(got[at, j, 2 * HALF :]))


def own_spots():
    r = lax.broadcasted_iota(jnp.int32, (HALF, HALF), 0)
    c = lax.broadcasted_iota(jnp.int32, (HALF, HALF), 1)
    inside = (r // 4 == c // 4) & (r < c)
    r, c = r % 4, c % 4
    return (
        inside & (r == 0),
        inside & (r == 1) & (c == 2),
        inside & (r == 1) & (c == 3),
        inside & (r == 2),
    )


def with_extras(square, spots, before, after, head, rest):
    for spot, value in zip(spots, (before, after, head, rest)):
        square = jnp.where(spot, jnp.broadcast_to(value, square.shape), square)
    return square


def unpack_kernel(at, keep, got, *refs):
    arrived, out, full = refs[:-2], refs[-2], refs[-1]
    r = lax.broadcasted_iota(jnp.int32, (HALF, HALF), 0)
    c = lax.broadcasted_iota(jnp.int32, (HALF, HALF), 1)
    spots = own_spots()
    for j in range(2):
        body = keep[at, j, : 2 * HALF] + got[at, j, : 2 * HALF].astype(F32)
        extras = keep[at, j, 2 * HALF :] + joined2(got[at, j, 2 * HALF :])
        for a in arrived:
            body = body + a[j, : 2 * HALF].astype(F32)
            extras = extras + joined2(a[j, 2 * HALF :])
        b, both = body[:HALF], body[HALF:]
        flipped = jnp.transpose(both)
        if j == 0:
            totals = extras[3:4]
        value = totals[:, j : j + 1]
        head = value.astype(BF).astype(F32)
        before = jnp.roll(extras[1:3], 1, axis=1)
        after = jnp.roll(extras[1:3], HALF - 1, axis=1)
        low = jnp.where(r >= c, both, flipped)
        high = jnp.where(
            r < c, both, jnp.where(r > c, flipped, jnp.broadcast_to(extras[0:1], (HALF, HALF)))
        )
        full[j, :HALF, :HALF] = with_extras(
            low, spots, before[0:1], after[0:1], head, value - head
        )
        full[j, :HALF, HALF:] = b
        full[j, HALF:, :HALF] = jnp.transpose(b)
        full[j, HALF:, HALF:] = with_extras(
            high, spots, before[1:2], after[1:2], head, value - head
        )
    sub = lax.broadcasted_iota(jnp.int32, (8, 2 * HALF), 0)
    for m in range(out.shape[0] // 2):
        t0, t1 = full[0, 8 * m : 8 * m + 8], full[1, 8 * m : 8 * m + 8]
        out[2 * m] = jnp.where(sub < 4, t0, jnp.roll(t1, 4, axis=0)).astype(BF)
        out[2 * m + 1] = jnp.where(sub < 4, jnp.roll(t0, 4, axis=0), t1).astype(BF)


def final_kernel(norm, every, arrived, gram, rhs, totals):
    at = 8 * lax.axis_index("z") + 2 * lax.axis_index("x") + lax.axis_index("c")
    sides = []
    for core in range(2):
        side = arrived[core].astype(F32)
        for k in range(1, arrived.shape[0] // 2):
            side = side + arrived[2 * k + core].astype(F32)
        sides.append(side)
    block = jnp.concatenate(sides, axis=0)
    shape = block.shape
    lane = lax.broadcasted_iota(jnp.int32, shape, 1)
    sub = lax.rem(lax.broadcasted_iota(jnp.int32, shape, 0), 4)
    wide = [
        jnp.broadcast_to(
            jnp.sum(jnp.where(lane == 4 * at + k, block, 0.0), axis=1, keepdims=True), shape
        )
        for k in range(4)
    ]
    out = block
    for r in range(4):
        for c in range(r + 1, 4):
            mirror = jnp.roll(wide[r], r - c, axis=0)
            out = jnp.where((sub == r) & (lane == 4 * at + c), mirror, out)
    out = out * (1.0 / norm)
    spread = jnp.where(
        lane == 0,
        wide[1],
        jnp.where(lane == 1, wide[2], jnp.where(lane == 2, wide[3], jnp.roll(wide[2], -1, axis=0))),
    )
    spread = spread * (1.0 / norm)
    for q in range(PG):
        gram[q] = out[4 * q : 4 * q + 4]
        rhs[q : q + 1, :] = spread[4 * q : 4 * q + 1, 0:4]
    for k in range(2):
        totals[k] = (wide[3][4 * k + 1, 0] + wide[3][4 * k + 2, 0]) * (1.0 / every)


def call(kernel, outs, scratch, operands, out_specs=None, in_specs=None, flops=None):
    vmem = pl.BlockSpec(memory_space=pltpu.VMEM)
    cost = None
    if flops:
        cost = pl.CostEstimate(flops=flops, bytes_accessed=0, transcendentals=0)
    return pl.pallas_call(
        kernel,
        out_shape=tuple(jax.ShapeDtypeStruct(s, d) for s, d in outs),
        in_specs=in_specs or [vmem] * len(operands),
        out_specs=out_specs or tuple([vmem] * len(outs)),
        scratch_shapes=scratch,
        cost_estimate=cost,
        compiler_params=pltpu.CompilerParams(vmem_limit_bytes=GRANT),
    )(*operands)


def swapped(value, axis, by):
    return lax.ppermute(value, axis, [(k, k ^ by) for k in range(lax.axis_size(axis))])


def across_cores(at, keep, got):
    (out,) = call(
        functools.partial(cores_kernel, at), [((2, 2 * HALF + 16, HALF), BF)], [], (keep, got)
    )
    return out


def reduced(basis, residual, sigma, counts, pulsar, ecorr):
    groups = lax.axis_size("psr")
    slots, rows, width = basis.shape[2:]
    ndp = lax.axis_size(("z", "x", "c"))
    norm = float(ndp * slots * rows)
    every = norm * groups * groups
    keep, send, *shared = first_terms(
        basis[0], residual[0], sigma[0], counts[0], pulsar[0], ecorr
    )
    got = swapped(send, "c", 1)
    keep_b, send_b = later_terms((0,), shared, shared[-1])
    mine = across_cores(0, keep, got)
    arrived = [swapped(mine, "psr", ORDER[0])]
    got_b = swapped(send_b, "c", 1)
    keep, send = later_terms((1, 2), shared, mine)
    got = swapped(send, "c", 1)
    mine = across_cores(0, keep_b, got_b)
    arrived.append(swapped(mine, "psr", ORDER[1]))
    mine = across_cores(0, keep, got)
    arrived.append(swapped(mine, "psr", ORDER[2]))
    (wire,) = call(
        functools.partial(unpack_kernel, 1),
        [((ndp, 8, width), BF)],
        [pltpu.VMEM((2, width, width), F32)],
        (keep, got, *arrived),
    )
    wire = lax.all_to_all(wire, ("z", "x", "c"), 0, 0, tiled=True)
    return call(
        functools.partial(final_kernel, norm, every),
        [((PG, width // ndp, width), F32), ((PG, width // ndp), F32), ((2,), F32)],
        [],
        (wire,),
        (
            pl.BlockSpec(memory_space=pltpu.VMEM),
            pl.BlockSpec(memory_space=pltpu.VMEM),
            pl.BlockSpec(memory_space=pltpu.SMEM),
        ),
    )


def solution(mesh):
    finer = Mesh(mesh.devices.reshape(8, 4, 2, mesh.shape["psr"]), AXES)
    in_specs = (
        P(AXES, None, None, None, None),
        P(AXES, None, None, None),
        P(AXES, None, None, None),
        P(AXES, None, None),
        P(AXES, None, None),
        P(),
    )
    out_specs = (P("psr", ("z", "x", "c"), None), P("psr", ("z", "x", "c")), P())
    return jax.shard_map(
        reduced, mesh=finer, in_specs=in_specs, out_specs=out_specs, check_vma=False
    )
```

profile of v0, /device:TPU:1, one launch (start us, length us, event | category | flops | bytes accessed | tf_op | source)
XLA Modules:
  0.0 45.8 jit_solution(3203989954970402350)
XLA Ops:
  0.6 2.4 %shard_map.85 = (f32[1,2,264,128]{3,2,1,0:T(8,128)S(1)}, bf16[1,2,272,128]{3,2,1,0:T(8,128)(2,1)S(1)}, bf16[3,8,128,256]{3,2,1,0:T(8,128)(2,1)S(1)}, f32[3,2,8,1...) custom-call(s32[4,8]{1,0:T(4,128)} %bitcast.8, ...), custom_call_target="tpu_custom_call" | custom-call | tf_op jit(solution)/shard_map/pallas_call | solution.py:349
  3.1 3.3 %collective-permute-start = (bf16[1,2,272,128]{3,2,1,0:T(8,128)(2,1)S(1)}, bf16[1,2,272,128]{3,2,1,0:T(8,128)(2,1)S(1)}, u32[]{:S(2)}, u32[]{:S(2)}) collective-permute-start(bf16[1,2,272,128]{3,2,1,0:T(8,128)(2,1)S(1)} %get-tuple-element.20), channel_id=1, source_target_pairs={{0,4},{4,0},{1,5},{5,1},{2,6},{6,2},{3,7},{7,3},{8,12},{12,8},{9,1... | collective-permute-start | bytes 417800 | tf_op jit(solution)/shard_map/ppermute | solution.py:361
  6.4 1.0 %collective-permute-done.got = bf16[1,2,272,128]{3,2,1,0:T(8,128)(2,1)S(1)} collective-permute-done((bf16[1,2,272,128]{3,2,1,0:T(8,128)(2,1)S(1)}, bf16[1,2,272,128]{3,2,1,0:T(8,128)(2,1)S(1)}, u32[]{:S(2)}, u32[]{:S(2)}) %collective-permute-start) | collective-permute-done | bytes 139296 | tf_op jit(solution)/shard_map/ppermute | solution.py:361
  7.4 1.8 %shard_map.87 = (f32[2,2,264,128]{3,2,1,0:T(8,128)S(1)}, bf16[2,2,272,128]{3,2,1,0:T(8,128)(2,1)S(1)}) custom-call(bf16[3,8,128,256]{3,2,1,0:T(8,128)(2,1)S(1)} %get-tuple-element.14.later, f32[3,2,8,128]{3,2,1,0:T(8,128)S(1)} %get-tuple-element.15.rows, f32[3,2,8,128]{3,2,1,0:T(8,128)S(1)} %get-tuple-element.16.wide, ...), custom_call_target="tpu_custom_call" | custom-call | flops 2000000000 | tf_op jit(solution)/shard_map/pallas_call | solution.py:349
  9.3 0.5 collective-permute-start.1
  9.7 1.1 %shard_map.88 = (f32[1,2,264,128]{3,2,1,0:T(8,128)S(1)}, bf16[1,2,272,128]{3,2,1,0:T(8,128)(2,1)S(1)}) custom-call(bf16[3,8,128,256]{3,2,1,0:T(8,128)(2,1)S(1)} %get-tuple-element.14.later, f32[3,2,8,128]{3,2,1,0:T(8,128)S(1)} %get-tuple-element.15.rows, f32[3,2,8,128]{3,2,1,0:T(8,128)S(1)} %get-tuple-element.16.wide, ...), custom_call_target="tpu_custom_call" | custom-call | flops 1000000000 | tf_op jit(solution)/shard_map/pallas_call | solution.py:349
  10.8 0.2 collective-permute-start.3
  11.0 1.2 %collective-permute-start.2 = (bf16[2,272,128]{2,1,0:T(8,128)(2,1)S(1)}, bf16[2,272,128]{2,1,0:T(8,128)(2,1)S(1)}, u32[]{:S(2)}, u32[]{:S(2)}) collective-permute-start(bf16[2,272,128]{2,1,0:T(8,128)(2,1)S(1)} %shard_map.86.after), channel_id=1, source_target_pairs={{0,2},{1,3},{2,0},{3,1},{4,6},{5,7},{6,4},{7,5},{8,10},{9,11},{10,... | collective-permute-start | bytes 417800 | tf_op jit(solution)/shard_map/ppermute | solution.py:361
  12.2 0.0 collective-permute-done.3.got
  12.3 0.5 %collective-permute-start.4 = (bf16[2,272,128]{2,1,0:T(8,128)(2,1)S(1)}, bf16[2,272,128]{2,1,0:T(8,128)(2,1)S(1)}, u32[]{:S(2)}, u32[]{:S(2)}) collective-permute-start(bf16[2,272,128]{2,1,0:T(8,128)(2,1)S(1)} %shard_map.89), channel_id=1, source_target_pairs={{0,1},{1,0},{2,3},{3,2},{4,5},{5,4},{6,7},{7,6},{8,9},{9,8},{10,11... | collective-permute-start | bytes 417800 | tf_op jit(solution)/shard_map/ppermute | solution.py:361
  12.7 0.0 collective-permute-done.1.got
  12.8 1.7 %collective-permute-start.5 = (bf16[2,272,128]{2,1,0:T(8,128)(2,1)S(1)}, bf16[2,272,128]{2,1,0:T(8,128)(2,1)S(1)}, u32[]{:S(2)}, u32[]{:S(2)}) collective-permute-start(bf16[2,272,128]{2,1,0:T(8,128)(2,1)S(1)} %shard_map.90), channel_id=1, source_target_pairs={{0,3},{1,2},{2,1},{3,0},{4,7},{5,6},{6,5},{7,4},{8,11},{9,10},{10,... | collective-permute-start | bytes 417800 | tf_op jit(solution)/shard_map/ppermute | solution.py:361
  14.5 2.9 %collective-permute-done.2.refs_0_ = bf16[2,272,128]{2,1,0:T(8,128)(2,1)S(1)} collective-permute-done((bf16[2,272,128]{2,1,0:T(8,128)(2,1)S(1)}, bf16[2,272,128]{2,1,0:T(8,128)(2,1)S(1)}, u32[]{:S(2)}, u32[]{:S(2)}) %collective-permute-start.2) | collective-permute-done | bytes 139296 | tf_op jit(solution)/shard_map/ppermute | solution.py:361
  17.4 1.6 %collective-permute-done.4.refs_1_ = bf16[2,272,128]{2,1,0:T(8,128)(2,1)S(1)} collective-permute-done((bf16[2,272,128]{2,1,0:T(8,128)(2,1)S(1)}, bf16[2,272,128]{2,1,0:T(8,128)(2,1)S(1)}, u32[]{:S(2)}, u32[]{:S(2)}) %collective-permute-start.4) | collective-permute-done | bytes 139296 | tf_op jit(solution)/shard_map/ppermute | solution.py:361
  19.0 1.8 %collective-permute-done.5.refs_2_ = bf16[2,272,128]{2,1,0:T(8,128)(2,1)S(1)} collective-permute-done((bf16[2,272,128]{2,1,0:T(8,128)(2,1)S(1)}, bf16[2,272,128]{2,1,0:T(8,128)(2,1)S(1)}, u32[]{:S(2)}, u32[]{:S(2)}) %collective-permute-start.5) | collective-permute-done | bytes 139296 | tf_op jit(solution)/shard_map/ppermute | solution.py:361
  20.8 0.3 shard_map.91
  21.1 23.9 %all_to_all.5.arrived = bf16[64,8,256]{2,1,0:T(8,128)(2,1)S(1)} all-to-all(bf16[64,8,256]{2,1,0:T(8,128)(2,1)S(1)} %shard_map.91), channel_id=1, replica_groups=mesh['z'=8,'x'=4,'c'=2,'psr'=4] {'z','x','c'}, dimensions={0} | all-to-all | bytes 524288 | tf_op jit(solution)/shard_map/all_to_all | solution.py:397
  45.0 0.8 %shard_map.92 = (f32[4,4,256]{2,1,0:T(4,128)}, f32[4,4]{1,0:T(4,128)}, f32[2]{0:T(128)}) custom-call(bf16[64,8,256]{2,1,0:T(8,128)(2,1)S(1)} %all_to_all.5.arrived), custom_call_target="tpu_custom_call" | custom-call | tf_op jit(solution)/shard_map/pallas_call | solution.py:349
  (3 shorter events, 0.1 us)
Async XLA Ops:
  3.1 4.3 %collective-permute-start = (bf16[1,2,272,128]{3,2,1,0:T(8,128)(2,1)S(1)}, bf16[1,2,272,128]{3,2,1,0:T(8,128)(2,1)S(1)}, u32[]{:S(2)}, u32[]{:S(2)}) collective-permute-start(bf16[1,2,272,128]{3,2,1,0:T(8,128)(2,1)S(1)} %get-tuple-element.20), channel_id=1, source_target_pairs={{0,4},{4,0},{1,5},{5,1},{2,6},{6,2},{3,7},{7,3},{8,12},{12,8},{9,1... | collective-permute-start | bytes 417800 | tf_op jit(solution)/shard_map/ppermute | solution.py:361
  9.3 3.5 %collective-permute-start.1 = (bf16[2,2,272,128]{3,2,1,0:T(8,128)(2,1)S(1)}, bf16[2,2,272,128]{3,2,1,0:T(8,128)(2,1)S(1)}, u32[]{:S(2)}, u32[]{:S(2)}) collective-permute-start(bf16[2,2,272,128]{3,2,1,0:T(8,128)(2,1)S(1)} %get-tuple-element.22), channel_id=1, source_target_pairs={{0,4},{4,0},{1,5},{5,1},{2,6},{6,2},{3,7},{7,3},{8,12},{12,8},{9,1... | collective-permute-start | bytes 835592 | tf_op jit(solution)/shard_map/ppermute | solution.py:361
  10.8 1.4 %collective-permute-start.3 = (bf16[1,2,272,128]{3,2,1,0:T(8,128)(2,1)S(1)}, bf16[1,2,272,128]{3,2,1,0:T(8,128)(2,1)S(1)}, u32[]{:S(2)}, u32[]{:S(2)}) collective-permute-start(bf16[1,2,272,128]{3,2,1,0:T(8,128)(2,1)S(1)} %get-tuple-element.24), channel_id=1, source_target_pairs={{0,4},{4,0},{1,5},{5,1},{2,6},{6,2},{3,7},{7,3},{8,12},{12,8},{9,1... | collective-permute-start | bytes 417800 | tf_op jit(solution)/shard_map/ppermute | solution.py:361
  11.0 6.4 %collective-permute-start.2 = (bf16[2,272,128]{2,1,0:T(8,128)(2,1)S(1)}, bf16[2,272,128]{2,1,0:T(8,128)(2,1)S(1)}, u32[]{:S(2)}, u32[]{:S(2)}) collective-permute-start(bf16[2,272,128]{2,1,0:T(8,128)(2,1)S(1)} %shard_map.86.after), channel_id=1, source_target_pairs={{0,2},{1,3},{2,0},{3,1},{4,6},{5,7},{6,4},{7,5},{8,10},{9,11},{10,... | collective-permute-start | bytes 417800 | tf_op jit(solution)/shard_map/ppermute | solution.py:361
  12.3 6.7 %collective-permute-start.4 = (bf16[2,272,128]{2,1,0:T(8,128)(2,1)S(1)}, bf16[2,272,128]{2,1,0:T(8,128)(2,1)S(1)}, u32[]{:S(2)}, u32[]{:S(2)}) collective-permute-start(bf16[2,272,128]{2,1,0:T(8,128)(2,1)S(1)} %shard_map.89), channel_id=1, source_target_pairs={{0,1},{1,0},{2,3},{3,2},{4,5},{5,4},{6,7},{7,6},{8,9},{9,8},{10,11... | collective-permute-start | bytes 417800 | tf_op jit(solution)/shard_map/ppermute | solution.py:361
  12.8 8.0 %collective-permute-start.5 = (bf16[2,272,128]{2,1,0:T(8,128)(2,1)S(1)}, bf16[2,272,128]{2,1,0:T(8,128)(2,1)S(1)}, u32[]{:S(2)}, u32[]{:S(2)}) collective-permute-start(bf16[2,272,128]{2,1,0:T(8,128)(2,1)S(1)} %shard_map.90), channel_id=1, source_target_pairs={{0,3},{1,2},{2,1},{3,0},{4,7},{5,6},{6,5},{7,4},{8,11},{9,10},{10,... | collective-permute-start | bytes 417800 | tf_op jit(solution)/shard_map/ppermute | solution.py:361
where the time goes:
time: 45.9 us; the launch traced here: 45.8 us
  blocking collectives  23.9 us (52%)
  starting transfers between devices  7.38 us (16%)
  waiting for transfers between devices  7.28 us (16%)
  Pallas kernels  6.49 us (14%)
  between operations  0.67 us (1%)
    all_to_all x1, blocking collectives, reduced(): wire = lax.all_to_all(wire, ('z', 'x', 'c'), 0, 0, tiled=True)  23.9 us
    ppermute x6, starting transfers between devices, swapped(): lax.ppermute(value, axis, [(k, k ^ by) for k in range(lax.axis_size(axis))])  7.38 us
    ppermute x6, waiting for transfers between devices, swapped(): lax.ppermute(value, axis, [(k, k ^ by) for k in range(lax.axis_size(axis))])  7.28 us
    pallas_call x8, Pallas kernels, call(): pl.pallas_call(kernel, out_shape=tuple((jax.ShapeDtypeStruct(s, d) for s,...  6.49 us
  transfers between devices with their start and end apart: 6, of which 4 were waited for; matrix products, arithmetic and copies ran while one was open for 0% of the time, Pallas kernels for 2%

commit v1 on v0

--- a/solution.py
+++ b/solution.py
@@ -139,6 +139,7 @@
     keep, send, later, rows_o, wide_o, member_o, totals_o,
     counts, pulsar, ecorr, sigma, residual, small_sems, buf, sems, acc, racc, rows_s, wide_s, member_s,
 ):
+    groups = counts.shape[0]
     y = lax.axis_index("psr")
     core = lax.axis_index("c")
     small = [
@@ -158,14 +159,15 @@
     copies = []
     for k, i in enumerate(ORDER):
         target = buf if k == 0 else later.at[k - 1]
-        copies.append(pltpu.make_async_copy(basis.at[y ^ i], target, sems.at[k]))
+        copies.append(pltpu.make_async_copy(basis.at[lax.rem(y + i, groups)], target, sems.at[k]))
         copies[-1].start()
     for copy in small:
         copy.wait()
     logdet, chi = 0.0, 0.0
     for k, i in enumerate(ORDER):
         places = (rows_s, wide_s, member_s, 0) if k == 0 else (rows_o, wide_o, member_o, k - 1)
-        part = prepare(places[3], y ^ i, counts, pulsar, ecorr, sigma, residual, *places[:3])
+        g = lax.rem(y + i, groups)
+        part = prepare(places[3], g, counts, pulsar, ecorr, sigma, residual, *places[:3])
         logdet, chi = logdet + part[0], chi + part[1]
     lane1 = lax.broadcasted_iota(jnp.int32, (1, HALF), 1)
     totals = jnp.where(
@@ -240,11 +242,17 @@
     )
 
 
-def cores_kernel(at, keep, got, out):
+def cores_kernel(at, relayed, keep, got, *refs):
+    extra = refs[0] if relayed is not None else None
     for j in range(2):
         body = keep[at, j, : 2 * HALF] + got[at, j, : 2 * HALF].astype(F32)
-        out[j, : 2 * HALF] = body.astype(BF)
-        out[j, 2 * HALF :] = split2(keep[at, j, 2 * HALF :] + joined2(got[at, j, 2 * HALF :]))
+        extras = keep[at, j, 2 * HALF :] + joined2(got[at, j, 2 * HALF :])
+        if relayed == j:
+            body = body + extra[: 2 * HALF].astype(F32)
+            extras = extras + joined2(extra[2 * HALF :])
+        out = refs[j] if relayed is None else refs[1].at[j]
+        out[: 2 * HALF] = body.astype(BF)
+        out[2 * HALF :] = split2(extras)
 
 
 def own_spots():
@@ -361,11 +369,16 @@
     return lax.ppermute(value, axis, [(k, k ^ by) for k in range(lax.axis_size(axis))])
 
 
-def across_cores(at, keep, got):
-    (out,) = call(
-        functools.partial(cores_kernel, at), [((2, 2 * HALF + 16, HALF), BF)], [], (keep, got)
-    )
-    return out
+def shifted(value, axis, by):
+    n = lax.axis_size(axis)
+    return lax.ppermute(value, axis, [(k, (k + by) % n) for k in range(n)])
+
+
+def across_cores(at, keep, got, relayed=None, extra=None):
+    wire = (2 * HALF + 16, HALF)
+    outs = [(wire, BF)] * 2 if relayed is None else [((2, *wire), BF)]
+    operands = (keep, got) if relayed is None else (keep, got, extra)
+    return call(functools.partial(cores_kernel, at, relayed), outs, [], operands)
 
 
 def reduced(basis, residual, sigma, counts, pulsar, ecorr):
@@ -379,15 +392,16 @@
     )
     got = swapped(send, "c", 1)
     keep_b, send_b = later_terms((0,), shared, shared[-1])
-    mine = across_cores(0, keep, got)
-    arrived = [swapped(mine, "psr", ORDER[0])]
+    up, down = across_cores(0, keep, got)
+    from_below = shifted(up, "psr", 1)
+    from_above = shifted(down, "psr", -1)
     got_b = swapped(send_b, "c", 1)
-    keep, send = later_terms((1, 2), shared, mine)
+    keep, send = later_terms((1, 2), shared, up)
     got = swapped(send, "c", 1)
-    mine = across_cores(0, keep_b, got_b)
-    arrived.append(swapped(mine, "psr", ORDER[1]))
-    mine = across_cores(0, keep, got)
-    arrived.append(swapped(mine, "psr", ORDER[2]))
+    (mine,) = across_cores(0, keep_b, got_b, 0, from_below)
+    arrived = [shifted(mine, "psr", 1)]
+    (mine,) = across_cores(0, keep, got, 1, from_above)
+    arrived.append(shifted(mine, "psr", -1))
     (wire,) = call(
         functools.partial(unpack_kernel, 1),
         [((ndp, 8, width), BF)],

time: 45.9 us -> 47.1 us (1.026)
  waiting for transfers between devices: 7.28 us -> 5 us
  starting transfers between devices: 7.38 us -> 9.46 us
  blocking collectives: 23.9 us -> 25.3 us
    ppermute x6 -> x3, waiting for transfers between devices: 7.28 us -> 1 us  [swapped(): lax.ppermute(value, axis, [(k, k ^ by) for k in range(lax.axis_size(axis))])]
    ppermute x0 -> x4, starting transfers between devices: none -> 5.49 us  [shifted(): return lax.ppermute(value, axis, [(k, (k + by) % n) for k in range(n)])]
    ppermute x0 -> x4, waiting for transfers between devices: none -> 4 us  [shifted(): return lax.ppermute(value, axis, [(k, (k + by) % n) for k in range(n)])]
    ppermute x6 -> x3, starting transfers between devices: 7.38 us -> 3.97 us  [swapped(): lax.ppermute(value, axis, [(k, k ^ by) for k in range(lax.axis_size(axis))])]
    all_to_all x1, blocking collectives: 23.9 us -> 25.3 us  [reduced(): wire = lax.all_to_all(wire, ('z', 'x', 'c'), 0, 0, tiled=True)]
  transfers between devices with their start and end apart: 6 -> 7, of which waited for: 4 -> 3; matrix products, arithmetic and copies ran while one was open for 0% -> 0% of each run, Pallas kernels for 2% -> 2%
where the time goes in v1:
time: 47.1 us; the launch traced here: 47 us
  blocking collectives  25.3 us (54%)
  starting transfers between devices  9.46 us (20%)
  Pallas kernels  6.53 us (14%)
  waiting for transfers between devices  5 us (11%)
  between operations  0.69 us (1%)
    all_to_all x1, blocking collectives, reduced(): wire = lax.all_to_all(wire, ('z', 'x', 'c'), 0, 0, tiled=True)  25.3 us
    pallas_call x8, Pallas kernels, call(): pl.pallas_call(kernel, out_shape=tuple((jax.ShapeDtypeStruct(s, d) for s,...  6.53 us
    ppermute x4, starting transfers between devices, shifted(): return lax.ppermute(value, axis, [(k, (k + by) % n) for k in range(n)])  5.49 us
    ppermute x4, waiting for transfers between devices, shifted(): return lax.ppermute(value, axis, [(k, (k + by) % n) for k in range(n)])  4 us
    ppermute x3, starting transfers between devices, swapped(): lax.ppermute(value, axis, [(k, k ^ by) for k in range(lax.axis_size(axis))])  3.97 us
    ppermute x3, waiting for transfers between devices, swapped(): lax.ppermute(value, axis, [(k, k ^ by) for k in range(lax.axis_size(axis))])  1 us
  transfers between devices with their start and end apart: 7, of which 3 were waited for; matrix products, arithmetic and copies ran while one was open for 0% of the time, Pallas kernels for 2%

profile of v1, /device:TPU:1, one launch (start us, length us, event | category | flops | bytes accessed | tf_op | source)
XLA Modules:
  0.0 47.0 jit_solution(12563890901514411661)
XLA Ops:
  0.6 2.5 %shard_map.85 = (f32[1,2,264,128]{3,2,1,0:T(8,128)S(1)}, bf16[1,2,272,128]{3,2,1,0:T(8,128)(2,1)S(1)}, bf16[3,8,128,256]{3,2,1,0:T(8,128)(2,1)S(1)}, f32[3,2,8,1...) custom-call(s32[4,8]{1,0:T(4,128)} %bitcast.8, ...), custom_call_target="tpu_custom_call" | custom-call | tf_op jit(solution)/shard_map/pallas_call | solution.py:357
  3.1 3.3 %collective-permute-start = (bf16[1,2,272,128]{3,2,1,0:T(8,128)(2,1)S(1)}, bf16[1,2,272,128]{3,2,1,0:T(8,128)(2,1)S(1)}, u32[]{:S(2)}, u32[]{:S(2)}) collective-permute-start(bf16[1,2,272,128]{3,2,1,0:T(8,128)(2,1)S(1)} %get-tuple-element.22), channel_id=1, source_target_pairs={{0,4},{4,0},{1,5},{5,1},{2,6},{6,2},{3,7},{7,3},{8,12},{12,8},{9,1... | collective-permute-start | bytes 417800 | tf_op jit(solution)/shard_map/ppermute | solution.py:369
  6.4 1.0 %collective-permute-done.got = bf16[1,2,272,128]{3,2,1,0:T(8,128)(2,1)S(1)} collective-permute-done((bf16[1,2,272,128]{3,2,1,0:T(8,128)(2,1)S(1)}, bf16[1,2,272,128]{3,2,1,0:T(8,128)(2,1)S(1)}, u32[]{:S(2)}, u32[]{:S(2)}) %collective-permute-start) | collective-permute-done | bytes 139296 | tf_op jit(solution)/shard_map/ppermute | solution.py:369
  7.4 1.9 %shard_map.87 = (f32[2,2,264,128]{3,2,1,0:T(8,128)S(1)}, bf16[2,2,272,128]{3,2,1,0:T(8,128)(2,1)S(1)}) custom-call(bf16[3,8,128,256]{3,2,1,0:T(8,128)(2,1)S(1)} %get-tuple-element.16.later, f32[3,2,8,128]{3,2,1,0:T(8,128)S(1)} %get-tuple-element.17.rows, f32[3,2,8,128]{3,2,1,0:T(8,128)S(1)} %get-tuple-element.18.wide, ...), custom_call_target="tpu_custom_call" | custom-call | flops 2000000000 | tf_op jit(solution)/shard_map/pallas_call | solution.py:357
  9.3 0.5 collective-permute-start.1
  9.8 1.1 %shard_map.88 = (f32[1,2,264,128]{3,2,1,0:T(8,128)S(1)}, bf16[1,2,272,128]{3,2,1,0:T(8,128)(2,1)S(1)}) custom-call(bf16[3,8,128,256]{3,2,1,0:T(8,128)(2,1)S(1)} %get-tuple-element.16.later, f32[3,2,8,128]{3,2,1,0:T(8,128)S(1)} %get-tuple-element.17.rows, f32[3,2,8,128]{3,2,1,0:T(8,128)S(1)} %get-tuple-element.18.wide, ...), custom_call_target="tpu_custom_call" | custom-call | flops 1000000000 | tf_op jit(solution)/shard_map/pallas_call | solution.py:357
  10.8 0.2 collective-permute-start.2
  11.0 0.0 collective-permute-start.3
  11.1 2.7 %collective-permute-start.5 = (bf16[272,128]{1,0:T(8,128)(2,1)S(1)}, bf16[272,128]{1,0:T(8,128)(2,1)S(1)}, u32[]{:S(2)}, u32[]{:S(2)}) collective-permute-start(bf16[272,128]{1,0:T(8,128)(2,1)S(1)} %get-tuple-element.28), channel_id=1, source_target_pairs={{0,3},{1,0},{2,1},{3,2},{4,7},{5,4},{6,5},{7,6},{8,11},{9,8},{10,9... | collective-permute-start | bytes 208904 | tf_op jit(solution)/shard_map/ppermute | solution.py:374
  13.7 0.0 collective-permute-done.2.got
  13.7 1.7 %collective-permute-done.3.refs_0_ = bf16[272,128]{1,0:T(8,128)(2,1)S(1)} collective-permute-done((bf16[272,128]{1,0:T(8,128)(2,1)S(1)}, bf16[272,128]{1,0:T(8,128)(2,1)S(1)}, u32[]{:S(2)}, u32[]{:S(2)}) %collective-permute-start.3) | collective-permute-done | bytes 69664 | tf_op jit(solution)/shard_map/ppermute | solution.py:374
  15.5 0.1 collective-permute-start.4
  15.6 0.0 collective-permute-done.5.refs_0_
  15.6 0.0 collective-permute-done.1.got
  15.6 2.7 %collective-permute-start.6 = (bf16[2,272,128]{2,1,0:T(8,128)(2,1)S(1)}, bf16[2,272,128]{2,1,0:T(8,128)(2,1)S(1)}, u32[]{:S(2)}, u32[]{:S(2)}) collective-permute-start(bf16[2,272,128]{2,1,0:T(8,128)(2,1)S(1)} %shard_map.90), channel_id=1, source_target_pairs={{0,3},{1,0},{2,1},{3,2},{4,7},{5,4},{6,5},{7,6},{8,11},{9,8},{10,9... | collective-permute-start | bytes 417800 | tf_op jit(solution)/shard_map/ppermute | solution.py:374
  18.3 2.3 %collective-permute-done.4.refs_0_ = bf16[2,272,128]{2,1,0:T(8,128)(2,1)S(1)} collective-permute-done((bf16[2,272,128]{2,1,0:T(8,128)(2,1)S(1)}, bf16[2,272,128]{2,1,0:T(8,128)(2,1)S(1)}, u32[]{:S(2)}, u32[]{:S(2)}) %collective-permute-start.4) | collective-permute-done | bytes 139296 | tf_op jit(solution)/shard_map/ppermute | solution.py:374
  20.7 0.0 collective-permute-done.6.refs_1_
  20.7 0.3 shard_map.91
  20.9 25.3 %all_to_all.5.arrived = bf16[64,8,256]{2,1,0:T(8,128)(2,1)S(1)} all-to-all(bf16[64,8,256]{2,1,0:T(8,128)(2,1)S(1)} %shard_map.91), channel_id=1, replica_groups=mesh['z'=8,'x'=4,'c'=2,'psr'=4] {'z','x','c'}, dimensions={0} | all-to-all | bytes 524288 | tf_op jit(solution)/shard_map/all_to_all | solution.py:411
  46.2 0.8 %shard_map.92 = (f32[4,4,256]{2,1,0:T(4,128)}, f32[4,4]{1,0:T(4,128)}, f32[2]{0:T(128)}) custom-call(bf16[64,8,256]{2,1,0:T(8,128)(2,1)S(1)} %all_to_all.5.arrived), custom_call_target="tpu_custom_call" | custom-call | tf_op jit(solution)/shard_map/pallas_call | solution.py:357
  (3 shorter events, 0.1 us)
Async XLA Ops:
  3.1 4.3 %collective-permute-start = (bf16[1,2,272,128]{3,2,1,0:T(8,128)(2,1)S(1)}, bf16[1,2,272,128]{3,2,1,0:T(8,128)(2,1)S(1)}, u32[]{:S(2)}, u32[]{:S(2)}) collective-permute-start(bf16[1,2,272,128]{3,2,1,0:T(8,128)(2,1)S(1)} %get-tuple-element.22), channel_id=1, source_target_pairs={{0,4},{4,0},{1,5},{5,1},{2,6},{6,2},{3,7},{7,3},{8,12},{12,8},{9,1... | collective-permute-start | bytes 417800 | tf_op jit(solution)/shard_map/ppermute | solution.py:369
  9.3 6.3 %collective-permute-start.1 = (bf16[2,2,272,128]{3,2,1,0:T(8,128)(2,1)S(1)}, bf16[2,2,272,128]{3,2,1,0:T(8,128)(2,1)S(1)}, u32[]{:S(2)}, u32[]{:S(2)}) collective-permute-start(bf16[2,2,272,128]{3,2,1,0:T(8,128)(2,1)S(1)} %get-tuple-element.25), channel_id=1, source_target_pairs={{0,4},{4,0},{1,5},{5,1},{2,6},{6,2},{3,7},{7,3},{8,12},{12,8},{9,1... | collective-permute-start | bytes 835592 | tf_op jit(solution)/shard_map/ppermute | solution.py:369
  10.8 2.9 %collective-permute-start.2 = (bf16[1,2,272,128]{3,2,1,0:T(8,128)(2,1)S(1)}, bf16[1,2,272,128]{3,2,1,0:T(8,128)(2,1)S(1)}, u32[]{:S(2)}, u32[]{:S(2)}) collective-permute-start(bf16[1,2,272,128]{3,2,1,0:T(8,128)(2,1)S(1)} %get-tuple-element.27), channel_id=1, source_target_pairs={{0,4},{4,0},{1,5},{5,1},{2,6},{6,2},{3,7},{7,3},{8,12},{12,8},{9,1... | collective-permute-start | bytes 417800 | tf_op jit(solution)/shard_map/ppermute | solution.py:369
  11.0 4.4 %collective-permute-start.3 = (bf16[272,128]{1,0:T(8,128)(2,1)S(1)}, bf16[272,128]{1,0:T(8,128)(2,1)S(1)}, u32[]{:S(2)}, u32[]{:S(2)}) collective-permute-start(bf16[272,128]{1,0:T(8,128)(2,1)S(1)} %get-tuple-element.23.after), channel_id=1, source_target_pairs={{0,1},{1,2},{2,3},{3,0},{4,5},{5,6},{6,7},{7,4},{8,9},{9,10},{10,1... | collective-permute-start | bytes 208904 | tf_op jit(solution)/shard_map/ppermute | solution.py:374
  11.1 4.5 %collective-permute-start.5 = (bf16[272,128]{1,0:T(8,128)(2,1)S(1)}, bf16[272,128]{1,0:T(8,128)(2,1)S(1)}, u32[]{:S(2)}, u32[]{:S(2)}) collective-permute-start(bf16[272,128]{1,0:T(8,128)(2,1)S(1)} %get-tuple-element.28), channel_id=1, source_target_pairs={{0,3},{1,0},{2,1},{3,2},{4,7},{5,4},{6,5},{7,6},{8,11},{9,8},{10,9... | collective-permute-start | bytes 208904 | tf_op jit(solution)/shard_map/ppermute | solution.py:374
  15.5 5.2 %collective-permute-start.4 = (bf16[2,272,128]{2,1,0:T(8,128)(2,1)S(1)}, bf16[2,272,128]{2,1,0:T(8,128)(2,1)S(1)}, u32[]{:S(2)}, u32[]{:S(2)}) collective-permute-start(bf16[2,272,128]{2,1,0:T(8,128)(2,1)S(1)} %shard_map.89), channel_id=1, source_target_pairs={{0,1},{1,2},{2,3},{3,0},{4,5},{5,6},{6,7},{7,4},{8,9},{9,10},{10,1... | collective-permute-start | bytes 417800 | tf_op jit(solution)/shard_map/ppermute | solution.py:374
  15.6 5.0 %collective-permute-start.6 = (bf16[2,272,128]{2,1,0:T(8,128)(2,1)S(1)}, bf16[2,272,128]{2,1,0:T(8,128)(2,1)S(1)}, u32[]{:S(2)}, u32[]{:S(2)}) collective-permute-start(bf16[2,272,128]{2,1,0:T(8,128)(2,1)S(1)} %shard_map.90), channel_id=1, source_target_pairs={{0,3},{1,0},{2,1},{3,2},{4,7},{5,4},{6,5},{7,6},{8,11},{9,8},{10,9... | collective-permute-start | bytes 417800 | tf_op jit(solution)/shard_map/ppermute | solution.py:374

commit v2 on v1

--- a/solution.py
+++ b/solution.py
@@ -306,10 +306,12 @@
             high, spots, before[1:2], after[1:2], head, value - head
         )
     sub = lax.broadcasted_iota(jnp.int32, (8, 2 * HALF), 0)
-    for m in range(out.shape[0] // 2):
+    n_x, n_z = lax.axis_size("x"), lax.axis_size("z")
+    for m in range(n_z * n_x):
+        to = 2 * ((m % n_x) * n_z + m // n_x)
         t0, t1 = full[0, 8 * m : 8 * m + 8], full[1, 8 * m : 8 * m + 8]
-        out[2 * m] = jnp.where(sub < 4, t0, jnp.roll(t1, 4, axis=0)).astype(BF)
-        out[2 * m + 1] = jnp.where(sub < 4, jnp.roll(t0, 4, axis=0), t1).astype(BF)
+        out[to] = jnp.where(sub < 4, t0, jnp.roll(t1, 4, axis=0)).astype(BF)
+        out[to + 1] = jnp.where(sub < 4, jnp.roll(t0, 4, axis=0), t1).astype(BF)
 
 
 def final_kernel(norm, every, arrived, gram, rhs, totals):
@@ -408,7 +410,7 @@
         [pltpu.VMEM((2, width, width), F32)],
         (keep, got, *arrived),
     )
-    wire = lax.all_to_all(wire, ("z", "x", "c"), 0, 0, tiled=True)
+    wire = lax.all_to_all(wire, ("x", "z", "c"), 0, 0, tiled=True)
     return call(
         functools.partial(final_kernel, norm, every),
         [((PG, width // ndp, width), F32), ((PG, width // ndp), F32), ((2,), F32)],

time: 47.1 us -> 46 us (0.977)
  blocking collectives: 25.3 us -> 24.2 us
    all_to_all x1, blocking collectives: 25.3 us -> 24.2 us  [reduced(): wire = lax.all_to_all(wire, ('x', 'z', 'c'), 0, 0, tiled=True)]
where the time goes in v2:
time: 46 us; the launch traced here: 45.9 us
  blocking collectives  24.2 us (53%)
  starting transfers between devices  9.46 us (21%)
  Pallas kernels  6.53 us (14%)
  waiting for transfers between devices  5 us (11%)
  between operations  0.69 us (2%)
    all_to_all x1, blocking collectives, reduced(): wire = lax.all_to_all(wire, ('x', 'z', 'c'), 0, 0, tiled=True)  24.2 us
    pallas_call x8, Pallas kernels, call(): pl.pallas_call(kernel, out_shape=tuple((jax.ShapeDtypeStruct(s, d) for s,...  6.53 us
    ppermute x4, starting transfers between devices, shifted(): return lax.ppermute(value, axis, [(k, (k + by) % n) for k in range(n)])  5.49 us
    ppermute x4, waiting for transfers between devices, shifted(): return lax.ppermute(value, axis, [(k, (k + by) % n) for k in range(n)])  4 us
    ppermute x3, starting transfers between devices, swapped(): lax.ppermute(value, axis, [(k, k ^ by) for k in range(lax.axis_size(axis))])  3.97 us
    ppermute x3, waiting for transfers between devices, swapped(): lax.ppermute(value, axis, [(k, k ^ by) for k in range(lax.axis_size(axis))])  1 us
  transfers between devices with their start and end apart: 7, of which 3 were waited for; matrix products, arithmetic and copies ran while one was open for 0% of the time, Pallas kernels for 2%

profile of v2, /device:TPU:1, one launch (start us, length us, event | category | flops | bytes accessed | tf_op | source)
XLA Modules:
  0.0 45.9 jit_solution(8769195207609501356)
XLA Ops:
  0.6 2.5 %shard_map.85 = (f32[1,2,264,128]{3,2,1,0:T(8,128)S(1)}, bf16[1,2,272,128]{3,2,1,0:T(8,128)(2,1)S(1)}, bf16[3,8,128,256]{3,2,1,0:T(8,128)(2,1)S(1)}, f32[3,2,8,1...) custom-call(s32[4,8]{1,0:T(4,128)} %bitcast.8, ...), custom_call_target="tpu_custom_call" | custom-call | tf_op jit(solution)/shard_map/pallas_call | solution.py:359
  3.1 3.3 %collective-permute-start = (bf16[1,2,272,128]{3,2,1,0:T(8,128)(2,1)S(1)}, bf16[1,2,272,128]{3,2,1,0:T(8,128)(2,1)S(1)}, u32[]{:S(2)}, u32[]{:S(2)}) collective-permute-start(bf16[1,2,272,128]{3,2,1,0:T(8,128)(2,1)S(1)} %get-tuple-element.22), channel_id=1, source_target_pairs={{0,4},{4,0},{1,5},{5,1},{2,6},{6,2},{3,7},{7,3},{8,12},{12,8},{9,1... | collective-permute-start | bytes 417800 | tf_op jit(solution)/shard_map/ppermute | solution.py:371
  6.4 1.0 %collective-permute-done.got = bf16[1,2,272,128]{3,2,1,0:T(8,128)(2,1)S(1)} collective-permute-done((bf16[1,2,272,128]{3,2,1,0:T(8,128)(2,1)S(1)}, bf16[1,2,272,128]{3,2,1,0:T(8,128)(2,1)S(1)}, u32[]{:S(2)}, u32[]{:S(2)}) %collective-permute-start) | collective-permute-done | bytes 139296 | tf_op jit(solution)/shard_map/ppermute | solution.py:371
  7.4 1.9 %shard_map.87 = (f32[2,2,264,128]{3,2,1,0:T(8,128)S(1)}, bf16[2,2,272,128]{3,2,1,0:T(8,128)(2,1)S(1)}) custom-call(bf16[3,8,128,256]{3,2,1,0:T(8,128)(2,1)S(1)} %get-tuple-element.16.later, f32[3,2,8,128]{3,2,1,0:T(8,128)S(1)} %get-tuple-element.17.rows, f32[3,2,8,128]{3,2,1,0:T(8,128)S(1)} %get-tuple-element.18.wide, ...), custom_call_target="tpu_custom_call" | custom-call | flops 2000000000 | tf_op jit(solution)/shard_map/pallas_call | solution.py:359
  9.3 0.5 collective-permute-start.1
  9.8 1.1 %shard_map.88 = (f32[1,2,264,128]{3,2,1,0:T(8,128)S(1)}, bf16[1,2,272,128]{3,2,1,0:T(8,128)(2,1)S(1)}) custom-call(bf16[3,8,128,256]{3,2,1,0:T(8,128)(2,1)S(1)} %get-tuple-element.16.later, f32[3,2,8,128]{3,2,1,0:T(8,128)S(1)} %get-tuple-element.17.rows, f32[3,2,8,128]{3,2,1,0:T(8,128)S(1)} %get-tuple-element.18.wide, ...), custom_call_target="tpu_custom_call" | custom-call | flops 1000000000 | tf_op jit(solution)/shard_map/pallas_call | solution.py:359
  10.8 0.2 collective-permute-start.2
  11.0 0.0 collective-permute-start.3
  11.1 2.7 %collective-permute-start.5 = (bf16[272,128]{1,0:T(8,128)(2,1)S(1)}, bf16[272,128]{1,0:T(8,128)(2,1)S(1)}, u32[]{:S(2)}, u32[]{:S(2)}) collective-permute-start(bf16[272,128]{1,0:T(8,128)(2,1)S(1)} %get-tuple-element.28), channel_id=1, source_target_pairs={{0,3},{1,0},{2,1},{3,2},{4,7},{5,4},{6,5},{7,6},{8,11},{9,8},{10,9... | collective-permute-start | bytes 208904 | tf_op jit(solution)/shard_map/ppermute | solution.py:376
  13.7 0.0 collective-permute-done.2.got
  13.7 1.7 %collective-permute-done.3.refs_0_ = bf16[272,128]{1,0:T(8,128)(2,1)S(1)} collective-permute-done((bf16[272,128]{1,0:T(8,128)(2,1)S(1)}, bf16[272,128]{1,0:T(8,128)(2,1)S(1)}, u32[]{:S(2)}, u32[]{:S(2)}) %collective-permute-start.3) | collective-permute-done | bytes 69664 | tf_op jit(solution)/shard_map/ppermute | solution.py:376
  15.5 0.1 collective-permute-start.4
  15.6 0.0 collective-permute-done.5.refs_0_
  15.6 0.0 collective-permute-done.1.got
  15.6 2.7 %collective-permute-start.6 = (bf16[2,272,128]{2,1,0:T(8,128)(2,1)S(1)}, bf16[2,272,128]{2,1,0:T(8,128)(2,1)S(1)}, u32[]{:S(2)}, u32[]{:S(2)}) collective-permute-start(bf16[2,272,128]{2,1,0:T(8,128)(2,1)S(1)} %shard_map.90), channel_id=1, source_target_pairs={{0,3},{1,0},{2,1},{3,2},{4,7},{5,4},{6,5},{7,6},{8,11},{9,8},{10,9... | collective-permute-start | bytes 417800 | tf_op jit(solution)/shard_map/ppermute | solution.py:376
  18.3 2.3 %collective-permute-done.4.refs_0_ = bf16[2,272,128]{2,1,0:T(8,128)(2,1)S(1)} collective-permute-done((bf16[2,272,128]{2,1,0:T(8,128)(2,1)S(1)}, bf16[2,272,128]{2,1,0:T(8,128)(2,1)S(1)}, u32[]{:S(2)}, u32[]{:S(2)}) %collective-permute-start.4) | collective-permute-done | bytes 139296 | tf_op jit(solution)/shard_map/ppermute | solution.py:376
  20.7 0.0 collective-permute-done.6.refs_1_
  20.7 0.3 shard_map.91
  20.9 24.2 %all_to_all.5.arrived = bf16[64,8,256]{2,1,0:T(8,128)(2,1)S(1)} all-to-all(bf16[64,8,256]{2,1,0:T(8,128)(2,1)S(1)} %shard_map.91), channel_id=1, replica_groups=mesh['z'=8,'x'=4,'c'=2,'psr'=4] {'x','z','c'}, dimensions={0} | all-to-all | bytes 524288 | tf_op jit(solution)/shard_map/all_to_all | solution.py:413
  45.1 0.8 %shard_map.92 = (f32[4,4,256]{2,1,0:T(4,128)}, f32[4,4]{1,0:T(4,128)}, f32[2]{0:T(128)}) custom-call(bf16[64,8,256]{2,1,0:T(8,128)(2,1)S(1)} %all_to_all.5.arrived), custom_call_target="tpu_custom_call" | custom-call | tf_op jit(solution)/shard_map/pallas_call | solution.py:359
  (3 shorter events, 0.1 us)
Async XLA Ops:
  3.1 4.3 %collective-permute-start = (bf16[1,2,272,128]{3,2,1,0:T(8,128)(2,1)S(1)}, bf16[1,2,272,128]{3,2,1,0:T(8,128)(2,1)S(1)}, u32[]{:S(2)}, u32[]{:S(2)}) collective-permute-start(bf16[1,2,272,128]{3,2,1,0:T(8,128)(2,1)S(1)} %get-tuple-element.22), channel_id=1, source_target_pairs={{0,4},{4,0},{1,5},{5,1},{2,6},{6,2},{3,7},{7,3},{8,12},{12,8},{9,1... | collective-permute-start | bytes 417800 | tf_op jit(solution)/shard_map/ppermute | solution.py:371
  9.3 6.3 %collective-permute-start.1 = (bf16[2,2,272,128]{3,2,1,0:T(8,128)(2,1)S(1)}, bf16[2,2,272,128]{3,2,1,0:T(8,128)(2,1)S(1)}, u32[]{:S(2)}, u32[]{:S(2)}) collective-permute-start(bf16[2,2,272,128]{3,2,1,0:T(8,128)(2,1)S(1)} %get-tuple-element.25), channel_id=1, source_target_pairs={{0,4},{4,0},{1,5},{5,1},{2,6},{6,2},{3,7},{7,3},{8,12},{12,8},{9,1... | collective-permute-start | bytes 835592 | tf_op jit(solution)/shard_map/ppermute | solution.py:371
  10.8 2.9 %collective-permute-start.2 = (bf16[1,2,272,128]{3,2,1,0:T(8,128)(2,1)S(1)}, bf16[1,2,272,128]{3,2,1,0:T(8,128)(2,1)S(1)}, u32[]{:S(2)}, u32[]{:S(2)}) collective-permute-start(bf16[1,2,272,128]{3,2,1,0:T(8,128)(2,1)S(1)} %get-tuple-element.27), channel_id=1, source_target_pairs={{0,4},{4,0},{1,5},{5,1},{2,6},{6,2},{3,7},{7,3},{8,12},{12,8},{9,1... | collective-permute-start | bytes 417800 | tf_op jit(solution)/shard_map/ppermute | solution.py:371
  11.0 4.4 %collective-permute-start.3 = (bf16[272,128]{1,0:T(8,128)(2,1)S(1)}, bf16[272,128]{1,0:T(8,128)(2,1)S(1)}, u32[]{:S(2)}, u32[]{:S(2)}) collective-permute-start(bf16[272,128]{1,0:T(8,128)(2,1)S(1)} %get-tuple-element.23.after), channel_id=1, source_target_pairs={{0,1},{1,2},{2,3},{3,0},{4,5},{5,6},{6,7},{7,4},{8,9},{9,10},{10,1... | collective-permute-start | bytes 208904 | tf_op jit(solution)/shard_map/ppermute | solution.py:376
  11.1 4.5 %collective-permute-start.5 = (bf16[272,128]{1,0:T(8,128)(2,1)S(1)}, bf16[272,128]{1,0:T(8,128)(2,1)S(1)}, u32[]{:S(2)}, u32[]{:S(2)}) collective-permute-start(bf16[272,128]{1,0:T(8,128)(2,1)S(1)} %get-tuple-element.28), channel_id=1, source_target_pairs={{0,3},{1,0},{2,1},{3,2},{4,7},{5,4},{6,5},{7,6},{8,11},{9,8},{10,9... | collective-permute-start | bytes 208904 | tf_op jit(solution)/shard_map/ppermute | solution.py:376
  15.5 5.2 %collective-permute-start.4 = (bf16[2,272,128]{2,1,0:T(8,128)(2,1)S(1)}, bf16[2,272,128]{2,1,0:T(8,128)(2,1)S(1)}, u32[]{:S(2)}, u32[]{:S(2)}) collective-permute-start(bf16[2,272,128]{2,1,0:T(8,128)(2,1)S(1)} %shard_map.89), channel_id=1, source_target_pairs={{0,1},{1,2},{2,3},{3,0},{4,5},{5,6},{6,7},{7,4},{8,9},{9,10},{10,1... | collective-permute-start | bytes 417800 | tf_op jit(solution)/shard_map/ppermute | solution.py:376
  15.6 5.0 %collective-permute-start.6 = (bf16[2,272,128]{2,1,0:T(8,128)(2,1)S(1)}, bf16[2,272,128]{2,1,0:T(8,128)(2,1)S(1)}, u32[]{:S(2)}, u32[]{:S(2)}) collective-permute-start(bf16[2,272,128]{2,1,0:T(8,128)(2,1)S(1)} %shard_map.90), channel_id=1, source_target_pairs={{0,3},{1,0},{2,1},{3,2},{4,7},{5,4},{6,5},{7,6},{8,11},{9,8},{10,9... | collective-permute-start | bytes 417800 | tf_op jit(solution)/shard_map/ppermute | solution.py:376

commit v3 on v2

--- a/solution.py
+++ b/solution.py
@@ -398,14 +398,16 @@
     from_below = shifted(up, "psr", 1)
     from_above = shifted(down, "psr", -1)
     got_b = swapped(send_b, "c", 1)
-    keep, send = later_terms((1, 2), shared, up)
+    keep_c, send_c = later_terms((1,), shared, up)
+    got_c = swapped(send_c, "c", 1)
+    keep, send = later_terms((2,), shared, keep_c)
     got = swapped(send, "c", 1)
     (mine,) = across_cores(0, keep_b, got_b, 0, from_below)
     arrived = [shifted(mine, "psr", 1)]
-    (mine,) = across_cores(0, keep, got, 1, from_above)
+    (mine,) = across_cores(0, keep_c, got_c, 1, from_above)
     arrived.append(shifted(mine, "psr", -1))
     (wire,) = call(
-        functools.partial(unpack_kernel, 1),
+        functools.partial(unpack_kernel, 0),
         [((ndp, 8, width), BF)],
         [pltpu.VMEM((2, width, width), F32)],
         (keep, got, *arrived),

time: 46 us -> 44.3 us (0.963)
  waiting for transfers between devices: 5 us -> 3.07 us
  starting transfers between devices: 9.46 us -> 10.2 us
  blocking collectives: 24.2 us -> 23.5 us
    ppermute x3 -> x4, waiting for transfers between devices: 1 us -> 0.01 us  [swapped(): lax.ppermute(value, axis, [(k, k ^ by) for k in range(lax.axis_size(axis))])]
    ppermute x4, waiting for transfers between devices: 4 us -> 3.05 us  [shifted(): return lax.ppermute(value, axis, [(k, (k + by) % n) for k in range(n)])]
    all_to_all x1, blocking collectives: 24.2 us -> 23.5 us  [reduced(): wire = lax.all_to_all(wire, ('x', 'z', 'c'), 0, 0, tiled=True)]
    ppermute x3 -> x4, starting transfers between devices: 3.97 us -> 4.7 us  [swapped(): lax.ppermute(value, axis, [(k, k ^ by) for k in range(lax.axis_size(axis))])]
    pallas_call x8 -> x9, Pallas kernels: 6.53 us -> 6.76 us  [call(): pl.pallas_call(kernel, out_shape=tuple((jax.ShapeDtypeStruct(s, d) for s,...]
  transfers between devices with their start and end apart: 7 -> 8, of which waited for: 3 -> 2; matrix products, arithmetic and copies ran while one was open for 0% -> 0% of each run, Pallas kernels for 2% -> 7%
where the time goes in v3:
time: 44.3 us; the launch traced here: 44.2 us
  blocking collectives  23.5 us (53%)
  starting transfers between devices  10.2 us (23%)
  Pallas kernels  6.76 us (15%)
  waiting for transfers between devices  3.07 us (7%)
  between operations  0.71 us (2%)
    all_to_all x1, blocking collectives, reduced(): wire = lax.all_to_all(wire, ('x', 'z', 'c'), 0, 0, tiled=True)  23.5 us
    pallas_call x9, Pallas kernels, call(): pl.pallas_call(kernel, out_shape=tuple((jax.ShapeDtypeStruct(s, d) for s,...  6.76 us
    ppermute x4, starting transfers between devices, shifted(): return lax.ppermute(value, axis, [(k, (k + by) % n) for k in range(n)])  5.49 us
    ppermute x4, starting transfers between devices, swapped(): lax.ppermute(value, axis, [(k, k ^ by) for k in range(lax.axis_size(axis))])  4.7 us
    ppermute x4, waiting for transfers between devices, shifted(): return lax.ppermute(value, axis, [(k, (k + by) % n) for k in range(n)])  3.05 us
  transfers between devices with their start and end apart: 8, of which 2 were waited for; matrix products, arithmetic and copies ran while one was open for 0% of the time, Pallas kernels for 7%

profile of v3, /device:TPU:1, one launch (start us, length us, event | category | flops | bytes accessed | tf_op | source)
XLA Modules:
  0.0 44.2 jit_solution(16562313273387771797)
XLA Ops:
  0.6 2.5 %shard_map.85 = (f32[1,2,264,128]{3,2,1,0:T(8,128)S(1)}, bf16[1,2,272,128]{3,2,1,0:T(8,128)(2,1)S(1)}, bf16[3,8,128,256]{3,2,1,0:T(8,128)(2,1)S(1)}, f32[3,2,8,1...) custom-call(s32[4,8]{1,0:T(4,128)} %bitcast.8, ...), custom_call_target="tpu_custom_call" | custom-call | tf_op jit(solution)/shard_map/pallas_call | solution.py:359
  3.1 3.3 %collective-permute-start = (bf16[1,2,272,128]{3,2,1,0:T(8,128)(2,1)S(1)}, bf16[1,2,272,128]{3,2,1,0:T(8,128)(2,1)S(1)}, u32[]{:S(2)}, u32[]{:S(2)}) collective-permute-start(bf16[1,2,272,128]{3,2,1,0:T(8,128)(2,1)S(1)} %get-tuple-element.24), channel_id=1, source_target_pairs={{0,4},{4,0},{1,5},{5,1},{2,6},{6,2},{3,7},{7,3},{8,12},{12,8},{9,1... | collective-permute-start | bytes 417800 | tf_op jit(solution)/shard_map/ppermute | solution.py:371
  6.4 1.1 %shard_map.89 = (f32[1,2,264,128]{3,2,1,0:T(8,128)S(1)}, bf16[1,2,272,128]{3,2,1,0:T(8,128)(2,1)S(1)}) custom-call(bf16[3,8,128,256]{3,2,1,0:T(8,128)(2,1)S(1)} %get-tuple-element.18.later, f32[3,2,8,128]{3,2,1,0:T(8,128)S(1)} %get-tuple-element.19.rows, f32[3,2,8,128]{3,2,1,0:T(8,128)S(1)} %get-tuple-element.20.wide, ...), custom_call_target="tpu_custom_call" | custom-call | flops 1000000000 | tf_op jit(solution)/shard_map/pallas_call | solution.py:359
  7.4 0.1 collective-permute-start.2
  7.5 0.0 collective-permute-done.got
  7.6 1.1 %shard_map.87 = (f32[1,2,264,128]{3,2,1,0:T(8,128)S(1)}, bf16[1,2,272,128]{3,2,1,0:T(8,128)(2,1)S(1)}) custom-call(bf16[3,8,128,256]{3,2,1,0:T(8,128)(2,1)S(1)} %get-tuple-element.18.later, f32[3,2,8,128]{3,2,1,0:T(8,128)S(1)} %get-tuple-element.19.rows, f32[3,2,8,128]{3,2,1,0:T(8,128)S(1)} %get-tuple-element.20.wide, ...), custom_call_target="tpu_custom_call" | custom-call | flops 1000000000 | tf_op jit(solution)/shard_map/pallas_call | solution.py:359
  8.7 0.6 %collective-permute-start.5 = (bf16[1,2,272,128]{3,2,1,0:T(8,128)(2,1)S(1)}, bf16[1,2,272,128]{3,2,1,0:T(8,128)(2,1)S(1)}, u32[]{:S(2)}, u32[]{:S(2)}) collective-permute-start(bf16[1,2,272,128]{3,2,1,0:T(8,128)(2,1)S(1)} %get-tuple-element.31), channel_id=1, source_target_pairs={{0,4},{4,0},{1,5},{5,1},{2,6},{6,2},{3,7},{7,3},{8,12},{12,8},{9,1... | collective-permute-start | bytes 417800 | tf_op jit(solution)/shard_map/ppermute | solution.py:371
  9.2 0.0 collective-permute-start.3
  9.2 2.7 %collective-permute-start.6 = (bf16[272,128]{1,0:T(8,128)(2,1)S(1)}, bf16[272,128]{1,0:T(8,128)(2,1)S(1)}, u32[]{:S(2)}, u32[]{:S(2)}) collective-permute-start(bf16[272,128]{1,0:T(8,128)(2,1)S(1)} %get-tuple-element.32), channel_id=1, source_target_pairs={{0,3},{1,0},{2,1},{3,2},{4,7},{5,4},{6,5},{7,6},{8,11},{9,8},{10,9... | collective-permute-start | bytes 208904 | tf_op jit(solution)/shard_map/ppermute | solution.py:376
  11.9 1.1 %shard_map.88 = (f32[1,2,264,128]{3,2,1,0:T(8,128)S(1)}, bf16[1,2,272,128]{3,2,1,0:T(8,128)(2,1)S(1)}) custom-call(bf16[3,8,128,256]{3,2,1,0:T(8,128)(2,1)S(1)} %get-tuple-element.18.later, f32[3,2,8,128]{3,2,1,0:T(8,128)S(1)} %get-tuple-element.19.rows, f32[3,2,8,128]{3,2,1,0:T(8,128)S(1)} %get-tuple-element.20.wide, ...), custom_call_target="tpu_custom_call" | custom-call | flops 1000000000 | tf_op jit(solution)/shard_map/pallas_call | solution.py:359
  13.0 0.7 %collective-permute-start.1 = (bf16[1,2,272,128]{3,2,1,0:T(8,128)(2,1)S(1)}, bf16[1,2,272,128]{3,2,1,0:T(8,128)(2,1)S(1)}, u32[]{:S(2)}, u32[]{:S(2)}) collective-permute-start(bf16[1,2,272,128]{3,2,1,0:T(8,128)(2,1)S(1)} %get-tuple-element.28), channel_id=1, source_target_pairs={{0,4},{4,0},{1,5},{5,1},{2,6},{6,2},{3,7},{7,3},{8,12},{12,8},{9,1... | collective-permute-start | bytes 417800 | tf_op jit(solution)/shard_map/ppermute | solution.py:371
  13.7 0.0 collective-permute-done.2.got
  13.7 0.4 collective-permute-done.3.refs_0_
  14.1 0.1 collective-permute-start.4
  14.2 0.0 collective-permute-done.6.refs_0_
  14.2 0.0 collective-permute-done.5.got
  14.2 0.1 shard_map.91
  14.3 2.7 %collective-permute-start.7 = (bf16[2,272,128]{2,1,0:T(8,128)(2,1)S(1)}, bf16[2,272,128]{2,1,0:T(8,128)(2,1)S(1)}, u32[]{:S(2)}, u32[]{:S(2)}) collective-permute-start(bf16[2,272,128]{2,1,0:T(8,128)(2,1)S(1)} %shard_map.91), channel_id=1, source_target_pairs={{0,3},{1,0},{2,1},{3,2},{4,7},{5,4},{6,5},{7,6},{8,11},{9,8},{10,9... | collective-permute-start | bytes 417800 | tf_op jit(solution)/shard_map/ppermute | solution.py:376
  17.0 0.0 collective-permute-done.1.got
  17.0 2.7 %collective-permute-done.4.refs_0_ = bf16[2,272,128]{2,1,0:T(8,128)(2,1)S(1)} collective-permute-done((bf16[2,272,128]{2,1,0:T(8,128)(2,1)S(1)}, bf16[2,272,128]{2,1,0:T(8,128)(2,1)S(1)}, u32[]{:S(2)}, u32[]{:S(2)}) %collective-permute-start.4) | collective-permute-done | bytes 139296 | tf_op jit(solution)/shard_map/ppermute | solution.py:376
  19.7 0.0 collective-permute-done.7.refs_1_
  19.7 0.3 shard_map.92
  20.0 23.5 %all_to_all.5.arrived = bf16[64,8,256]{2,1,0:T(8,128)(2,1)S(1)} all-to-all(bf16[64,8,256]{2,1,0:T(8,128)(2,1)S(1)} %shard_map.92), channel_id=1, replica_groups=mesh['z'=8,'x'=4,'c'=2,'psr'=4] {'x','z','c'}, dimensions={0} | all-to-all | bytes 524288 | tf_op jit(solution)/shard_map/all_to_all | solution.py:415
  43.4 0.8 %shard_map.93 = (f32[4,4,256]{2,1,0:T(4,128)}, f32[4,4]{1,0:T(4,128)}, f32[2]{0:T(128)}) custom-call(bf16[64,8,256]{2,1,0:T(8,128)(2,1)S(1)} %all_to_all.5.arrived), custom_call_target="tpu_custom_call" | custom-call | tf_op jit(solution)/shard_map/pallas_call | solution.py:359
  (2 shorter events, 0.1 us)
Async XLA Ops:
  3.1 4.5 %collective-permute-start = (bf16[1,2,272,128]{3,2,1,0:T(8,128)(2,1)S(1)}, bf16[1,2,272,128]{3,2,1,0:T(8,128)(2,1)S(1)}, u32[]{:S(2)}, u32[]{:S(2)}) collective-permute-start(bf16[1,2,272,128]{3,2,1,0:T(8,128)(2,1)S(1)} %get-tuple-element.24), channel_id=1, source_target_pairs={{0,4},{4,0},{1,5},{5,1},{2,6},{6,2},{3,7},{7,3},{8,12},{12,8},{9,1... | collective-permute-start | bytes 417800 | tf_op jit(solution)/shard_map/ppermute | solution.py:371
  7.4 6.3 %collective-permute-start.2 = (bf16[1,2,272,128]{3,2,1,0:T(8,128)(2,1)S(1)}, bf16[1,2,272,128]{3,2,1,0:T(8,128)(2,1)S(1)}, u32[]{:S(2)}, u32[]{:S(2)}) collective-permute-start(bf16[1,2,272,128]{3,2,1,0:T(8,128)(2,1)S(1)} %get-tuple-element.30), channel_id=1, source_target_pairs={{0,4},{4,0},{1,5},{5,1},{2,6},{6,2},{3,7},{7,3},{8,12},{12,8},{9,1... | collective-permute-start | bytes 417800 | tf_op jit(solution)/shard_map/ppermute | solution.py:371
  8.7 5.6 %collective-permute-start.5 = (bf16[1,2,272,128]{3,2,1,0:T(8,128)(2,1)S(1)}, bf16[1,2,272,128]{3,2,1,0:T(8,128)(2,1)S(1)}, u32[]{:S(2)}, u32[]{:S(2)}) collective-permute-start(bf16[1,2,272,128]{3,2,1,0:T(8,128)(2,1)S(1)} %get-tuple-element.31), channel_id=1, source_target_pairs={{0,4},{4,0},{1,5},{5,1},{2,6},{6,2},{3,7},{7,3},{8,12},{12,8},{9,1... | collective-permute-start | bytes 417800 | tf_op jit(solution)/shard_map/ppermute | solution.py:371
  9.2 4.9 %collective-permute-start.3 = (bf16[272,128]{1,0:T(8,128)(2,1)S(1)}, bf16[272,128]{1,0:T(8,128)(2,1)S(1)}, u32[]{:S(2)}, u32[]{:S(2)}) collective-permute-start(bf16[272,128]{1,0:T(8,128)(2,1)S(1)} %get-tuple-element.25.after), channel_id=1, source_target_pairs={{0,1},{1,2},{2,3},{3,0},{4,5},{5,6},{6,7},{7,4},{8,9},{9,10},{10,1... | collective-permute-start | bytes 208904 | tf_op jit(solution)/shard_map/ppermute | solution.py:376
  9.2 5.0 %collective-permute-start.6 = (bf16[272,128]{1,0:T(8,128)(2,1)S(1)}, bf16[272,128]{1,0:T(8,128)(2,1)S(1)}, u32[]{:S(2)}, u32[]{:S(2)}) collective-permute-start(bf16[272,128]{1,0:T(8,128)(2,1)S(1)} %get-tuple-element.32), channel_id=1, source_target_pairs={{0,3},{1,0},{2,1},{3,2},{4,7},{5,4},{6,5},{7,6},{8,11},{9,8},{10,9... | collective-permute-start | bytes 208904 | tf_op jit(solution)/shard_map/ppermute | solution.py:376
  13.0 4.1 %collective-permute-start.1 = (bf16[1,2,272,128]{3,2,1,0:T(8,128)(2,1)S(1)}, bf16[1,2,272,128]{3,2,1,0:T(8,128)(2,1)S(1)}, u32[]{:S(2)}, u32[]{:S(2)}) collective-permute-start(bf16[1,2,272,128]{3,2,1,0:T(8,128)(2,1)S(1)} %get-tuple-element.28), channel_id=1, source_target_pairs={{0,4},{4,0},{1,5},{5,1},{2,6},{6,2},{3,7},{7,3},{8,12},{12,8},{9,1... | collective-permute-start | bytes 417800 | tf_op jit(solution)/shard_map/ppermute | solution.py:371
  14.1 5.6 %collective-permute-start.4 = (bf16[2,272,128]{2,1,0:T(8,128)(2,1)S(1)}, bf16[2,272,128]{2,1,0:T(8,128)(2,1)S(1)}, u32[]{:S(2)}, u32[]{:S(2)}) collective-permute-start(bf16[2,272,128]{2,1,0:T(8,128)(2,1)S(1)} %shard_map.90), channel_id=1, source_target_pairs={{0,1},{1,2},{2,3},{3,0},{4,5},{5,6},{6,7},{7,4},{8,9},{9,10},{10,1... | collective-permute-start | bytes 417800 | tf_op jit(solution)/shard_map/ppermute | solution.py:376
  14.3 5.4 %collective-permute-start.7 = (bf16[2,272,128]{2,1,0:T(8,128)(2,1)S(1)}, bf16[2,272,128]{2,1,0:T(8,128)(2,1)S(1)}, u32[]{:S(2)}, u32[]{:S(2)}) collective-permute-start(bf16[2,272,128]{2,1,0:T(8,128)(2,1)S(1)} %shard_map.91), channel_id=1, source_target_pairs={{0,3},{1,0},{2,1},{3,2},{4,7},{5,4},{6,5},{7,6},{8,11},{9,8},{10,9... | collective-permute-start | bytes 417800 | tf_op jit(solution)/shard_map/ppermute | solution.py:376

commit v4 on v3

--- a/solution.py
+++ b/solution.py
@@ -131,7 +131,7 @@
         else:
             send[at_out, at - 2, 0:HALF, :] = b.astype(BF)
             send[at_out, at - 2, HALF : 2 * HALF, :] = both.astype(BF)
-            send[at_out, at - 2, 2 * HALF :, :] = split2(extras)
+            send[at_out, at - 2, 2 * HALF :, :] = split2(extras[:4])
 
 
 def first_kernel(
@@ -154,13 +154,15 @@
             )
         )
     ]
-    for copy in small:
-        copy.start()
     copies = []
     for k, i in enumerate(ORDER):
         target = buf if k == 0 else later.at[k - 1]
         copies.append(pltpu.make_async_copy(basis.at[lax.rem(y + i, groups)], target, sems.at[k]))
-        copies[-1].start()
+    copies[0].start()
+    for copy in small:
+        copy.start()
+    for copy in copies[1:]:
+        copy.start()
     for copy in small:
         copy.wait()
     logdet, chi = 0.0, 0.0
@@ -191,7 +193,7 @@
 
 
 def packs(n):
-    return [((n, 2, 2 * HALF + 8, HALF), F32), ((n, 2, 2 * HALF + 16, HALF), BF)]
+    return [((n, 2, 2 * HALF + 8, HALF), F32), ((n, 2, 2 * HALF + 8, HALF), BF)]
 
 
 def accumulators(width):
@@ -246,7 +248,7 @@
     extra = refs[0] if relayed is not None else None
     for j in range(2):
         body = keep[at, j, : 2 * HALF] + got[at, j, : 2 * HALF].astype(F32)
-        extras = keep[at, j, 2 * HALF :] + joined2(got[at, j, 2 * HALF :])
+        extras = keep[at, j, 2 * HALF : 2 * HALF + 4] + joined2(got[at, j, 2 * HALF :])
         if relayed == j:
             body = body + extra[: 2 * HALF].astype(F32)
             extras = extras + joined2(extra[2 * HALF :])
@@ -281,7 +283,7 @@
     spots = own_spots()
     for j in range(2):
         body = keep[at, j, : 2 * HALF] + got[at, j, : 2 * HALF].astype(F32)
-        extras = keep[at, j, 2 * HALF :] + joined2(got[at, j, 2 * HALF :])
+        extras = keep[at, j, 2 * HALF : 2 * HALF + 4] + joined2(got[at, j, 2 * HALF :])
         for a in arrived:
             body = body + a[j, : 2 * HALF].astype(F32)
             extras = extras + joined2(a[j, 2 * HALF :])
@@ -377,7 +379,7 @@
 
 
 def across_cores(at, keep, got, relayed=None, extra=None):
-    wire = (2 * HALF + 16, HALF)
+    wire = (2 * HALF + 8, HALF)
     outs = [(wire, BF)] * 2 if relayed is None else [((2, *wire), BF)]
     operands = (keep, got) if relayed is None else (keep, got, extra)
     return call(functools.partial(cores_kernel, at, relayed), outs, [], operands)

time: 44.3 us -> 44.2 us (level)
  no operation moved by 1% of the time
where the time goes in v4:
time: 44.2 us; the launch traced here: 44 us
  blocking collectives  23.5 us (53%)
  starting transfers between devices  10.2 us (23%)
  Pallas kernels  6.73 us (15%)
  waiting for transfers between devices  2.95 us (7%)
  between operations  0.71 us (2%)
    all_to_all x1, blocking collectives, reduced(): wire = lax.all_to_all(wire, ('x', 'z', 'c'), 0, 0, tiled=True)  23.5 us
    pallas_call x9, Pallas kernels, call(): pl.pallas_call(kernel, out_shape=tuple((jax.ShapeDtypeStruct(s, d) for s,...  6.73 us
    ppermute x4, starting transfers between devices, shifted(): return lax.ppermute(value, axis, [(k, (k + by) % n) for k in range(n)])  5.49 us
    ppermute x4, starting transfers between devices, swapped(): lax.ppermute(value, axis, [(k, k ^ by) for k in range(lax.axis_size(axis))])  4.7 us
    ppermute x4, waiting for transfers between devices, shifted(): return lax.ppermute(value, axis, [(k, (k + by) % n) for k in range(n)])  2.94 us
  transfers between devices with their start and end apart: 8, of which 2 were waited for; matrix products, arithmetic and copies ran while one was open for 0% of the time, Pallas kernels for 7%

profile of v4, /device:TPU:1, one launch (start us, length us, event | category | flops | bytes accessed | tf_op | source)
XLA Modules:
  0.0 44.0 jit_solution(4753472534786418497)
XLA Ops:
  0.6 2.5 %shard_map.85 = (f32[1,2,264,128]{3,2,1,0:T(8,128)S(1)}, bf16[1,2,264,128]{3,2,1,0:T(8,128)(2,1)S(1)}, bf16[3,8,128,256]{3,2,1,0:T(8,128)(2,1)S(1)}, f32[3,2,8,1...) custom-call(s32[4,8]{1,0:T(4,128)} %bitcast.8, ...), custom_call_target="tpu_custom_call" | custom-call | tf_op jit(solution)/shard_map/pallas_call | solution.py:361
  3.1 3.3 %collective-permute-start = (bf16[1,2,264,128]{3,2,1,0:T(8,128)(2,1)S(1)}, bf16[1,2,264,128]{3,2,1,0:T(8,128)(2,1)S(1)}, u32[]{:S(2)}, u32[]{:S(2)}) collective-permute-start(bf16[1,2,264,128]{3,2,1,0:T(8,128)(2,1)S(1)} %get-tuple-element.24), channel_id=1, source_target_pairs={{0,4},{4,0},{1,5},{5,1},{2,6},{6,2},{3,7},{7,3},{8,12},{12,8},{9,1... | collective-permute-start | bytes 405512 | tf_op jit(solution)/shard_map/ppermute | solution.py:373
  6.4 1.0 %shard_map.89 = (f32[1,2,264,128]{3,2,1,0:T(8,128)S(1)}, bf16[1,2,264,128]{3,2,1,0:T(8,128)(2,1)S(1)}) custom-call(bf16[3,8,128,256]{3,2,1,0:T(8,128)(2,1)S(1)} %get-tuple-element.18.later, f32[3,2,8,128]{3,2,1,0:T(8,128)S(1)} %get-tuple-element.19.rows, f32[3,2,8,128]{3,2,1,0:T(8,128)S(1)} %get-tuple-element.20.wide, ...), custom_call_target="tpu_custom_call" | custom-call | flops 1000000000 | tf_op jit(solution)/shard_map/pallas_call | solution.py:361
  7.4 0.1 collective-permute-start.2
  7.5 0.0 collective-permute-done.got
  7.6 1.0 %shard_map.87 = (f32[1,2,264,128]{3,2,1,0:T(8,128)S(1)}, bf16[1,2,264,128]{3,2,1,0:T(8,128)(2,1)S(1)}) custom-call(bf16[3,8,128,256]{3,2,1,0:T(8,128)(2,1)S(1)} %get-tuple-element.18.later, f32[3,2,8,128]{3,2,1,0:T(8,128)S(1)} %get-tuple-element.19.rows, f32[3,2,8,128]{3,2,1,0:T(8,128)S(1)} %get-tuple-element.20.wide, ...), custom_call_target="tpu_custom_call" | custom-call | flops 1000000000 | tf_op jit(solution)/shard_map/pallas_call | solution.py:361
  8.6 0.6 %collective-permute-start.5 = (bf16[1,2,264,128]{3,2,1,0:T(8,128)(2,1)S(1)}, bf16[1,2,264,128]{3,2,1,0:T(8,128)(2,1)S(1)}, u32[]{:S(2)}, u32[]{:S(2)}) collective-permute-start(bf16[1,2,264,128]{3,2,1,0:T(8,128)(2,1)S(1)} %get-tuple-element.31), channel_id=1, source_target_pairs={{0,4},{4,0},{1,5},{5,1},{2,6},{6,2},{3,7},{7,3},{8,12},{12,8},{9,1... | collective-permute-start | bytes 405512 | tf_op jit(solution)/shard_map/ppermute | solution.py:373
  9.2 0.0 collective-permute-start.3
  9.2 2.7 %collective-permute-start.6 = (bf16[264,128]{1,0:T(8,128)(2,1)S(1)}, bf16[264,128]{1,0:T(8,128)(2,1)S(1)}, u32[]{:S(2)}, u32[]{:S(2)}) collective-permute-start(bf16[264,128]{1,0:T(8,128)(2,1)S(1)} %get-tuple-element.32), channel_id=1, source_target_pairs={{0,3},{1,0},{2,1},{3,2},{4,7},{5,4},{6,5},{7,6},{8,11},{9,8},{10,9... | collective-permute-start | bytes 202760 | tf_op jit(solution)/shard_map/ppermute | solution.py:378
  11.9 1.0 %shard_map.88 = (f32[1,2,264,128]{3,2,1,0:T(8,128)S(1)}, bf16[1,2,264,128]{3,2,1,0:T(8,128)(2,1)S(1)}) custom-call(bf16[3,8,128,256]{3,2,1,0:T(8,128)(2,1)S(1)} %get-tuple-element.18.later, f32[3,2,8,128]{3,2,1,0:T(8,128)S(1)} %get-tuple-element.19.rows, f32[3,2,8,128]{3,2,1,0:T(8,128)S(1)} %get-tuple-element.20.wide, ...), custom_call_target="tpu_custom_call" | custom-call | flops 1000000000 | tf_op jit(solution)/shard_map/pallas_call | solution.py:361
  12.9 0.7 %collective-permute-start.1 = (bf16[1,2,264,128]{3,2,1,0:T(8,128)(2,1)S(1)}, bf16[1,2,264,128]{3,2,1,0:T(8,128)(2,1)S(1)}, u32[]{:S(2)}, u32[]{:S(2)}) collective-permute-start(bf16[1,2,264,128]{3,2,1,0:T(8,128)(2,1)S(1)} %get-tuple-element.28), channel_id=1, source_target_pairs={{0,4},{4,0},{1,5},{5,1},{2,6},{6,2},{3,7},{7,3},{8,12},{12,8},{9,1... | collective-permute-start | bytes 405512 | tf_op jit(solution)/shard_map/ppermute | solution.py:373
  13.7 0.0 collective-permute-done.2.got
  13.7 0.3 collective-permute-done.3.refs_0_
  14.1 0.1 collective-permute-start.4
  14.2 0.0 collective-permute-done.6.refs_0_
  14.2 0.0 collective-permute-done.5.got
  14.2 0.1 shard_map.91
  14.2 2.7 %collective-permute-start.7 = (bf16[2,264,128]{2,1,0:T(8,128)(2,1)S(1)}, bf16[2,264,128]{2,1,0:T(8,128)(2,1)S(1)}, u32[]{:S(2)}, u32[]{:S(2)}) collective-permute-start(bf16[2,264,128]{2,1,0:T(8,128)(2,1)S(1)} %shard_map.91), channel_id=1, source_target_pairs={{0,3},{1,0},{2,1},{3,2},{4,7},{5,4},{6,5},{7,6},{8,11},{9,8},{10,9... | collective-permute-start | bytes 405512 | tf_op jit(solution)/shard_map/ppermute | solution.py:378
  17.0 0.0 collective-permute-done.1.got
  17.0 2.6 %collective-permute-done.4.refs_0_ = bf16[2,264,128]{2,1,0:T(8,128)(2,1)S(1)} collective-permute-done((bf16[2,264,128]{2,1,0:T(8,128)(2,1)S(1)}, bf16[2,264,128]{2,1,0:T(8,128)(2,1)S(1)}, u32[]{:S(2)}, u32[]{:S(2)}) %collective-permute-start.4) | collective-permute-done | bytes 135200 | tf_op jit(solution)/shard_map/ppermute | solution.py:378
  19.5 0.0 collective-permute-done.7.refs_1_
  19.6 0.3 shard_map.92
  19.8 23.5 %all_to_all.5.arrived = bf16[64,8,256]{2,1,0:T(8,128)(2,1)S(1)} all-to-all(bf16[64,8,256]{2,1,0:T(8,128)(2,1)S(1)} %shard_map.92), channel_id=1, replica_groups=mesh['z'=8,'x'=4,'c'=2,'psr'=4] {'x','z','c'}, dimensions={0} | all-to-all | bytes 524288 | tf_op jit(solution)/shard_map/all_to_all | solution.py:417
  43.3 0.8 %shard_map.93 = (f32[4,4,256]{2,1,0:T(4,128)}, f32[4,4]{1,0:T(4,128)}, f32[2]{0:T(128)}) custom-call(bf16[64,8,256]{2,1,0:T(8,128)(2,1)S(1)} %all_to_all.5.arrived), custom_call_target="tpu_custom_call" | custom-call | tf_op jit(solution)/shard_map/pallas_call | solution.py:361
  (2 shorter events, 0.1 us)
Async XLA Ops:
  3.1 4.4 %collective-permute-start = (bf16[1,2,264,128]{3,2,1,0:T(8,128)(2,1)S(1)}, bf16[1,2,264,128]{3,2,1,0:T(8,128)(2,1)S(1)}, u32[]{:S(2)}, u32[]{:S(2)}) collective-permute-start(bf16[1,2,264,128]{3,2,1,0:T(8,128)(2,1)S(1)} %get-tuple-element.24), channel_id=1, source_target_pairs={{0,4},{4,0},{1,5},{5,1},{2,6},{6,2},{3,7},{7,3},{8,12},{12,8},{9,1... | collective-permute-start | bytes 405512 | tf_op jit(solution)/shard_map/ppermute | solution.py:373
  7.4 6.2 %collective-permute-start.2 = (bf16[1,2,264,128]{3,2,1,0:T(8,128)(2,1)S(1)}, bf16[1,2,264,128]{3,2,1,0:T(8,128)(2,1)S(1)}, u32[]{:S(2)}, u32[]{:S(2)}) collective-permute-start(bf16[1,2,264,128]{3,2,1,0:T(8,128)(2,1)S(1)} %get-tuple-element.30), channel_id=1, source_target_pairs={{0,4},{4,0},{1,5},{5,1},{2,6},{6,2},{3,7},{7,3},{8,12},{12,8},{9,1... | collective-permute-start | bytes 405512 | tf_op jit(solution)/shard_map/ppermute | solution.py:373
  8.6 5.5 %collective-permute-start.5 = (bf16[1,2,264,128]{3,2,1,0:T(8,128)(2,1)S(1)}, bf16[1,2,264,128]{3,2,1,0:T(8,128)(2,1)S(1)}, u32[]{:S(2)}, u32[]{:S(2)}) collective-permute-start(bf16[1,2,264,128]{3,2,1,0:T(8,128)(2,1)S(1)} %get-tuple-element.31), channel_id=1, source_target_pairs={{0,4},{4,0},{1,5},{5,1},{2,6},{6,2},{3,7},{7,3},{8,12},{12,8},{9,1... | collective-permute-start | bytes 405512 | tf_op jit(solution)/shard_map/ppermute | solution.py:373
  9.2 4.8 %collective-permute-start.3 = (bf16[264,128]{1,0:T(8,128)(2,1)S(1)}, bf16[264,128]{1,0:T(8,128)(2,1)S(1)}, u32[]{:S(2)}, u32[]{:S(2)}) collective-permute-start(bf16[264,128]{1,0:T(8,128)(2,1)S(1)} %get-tuple-element.25.after), channel_id=1, source_target_pairs={{0,1},{1,2},{2,3},{3,0},{4,5},{5,6},{6,7},{7,4},{8,9},{9,10},{10,1... | collective-permute-start | bytes 202760 | tf_op jit(solution)/shard_map/ppermute | solution.py:378
  9.2 5.0 %collective-permute-start.6 = (bf16[264,128]{1,0:T(8,128)(2,1)S(1)}, bf16[264,128]{1,0:T(8,128)(2,1)S(1)}, u32[]{:S(2)}, u32[]{:S(2)}) collective-permute-start(bf16[264,128]{1,0:T(8,128)(2,1)S(1)} %get-tuple-element.32), channel_id=1, source_target_pairs={{0,3},{1,0},{2,1},{3,2},{4,7},{5,4},{6,5},{7,6},{8,11},{9,8},{10,9... | collective-permute-start | bytes 202760 | tf_op jit(solution)/shard_map/ppermute | solution.py:378
  12.9 4.0 %collective-permute-start.1 = (bf16[1,2,264,128]{3,2,1,0:T(8,128)(2,1)S(1)}, bf16[1,2,264,128]{3,2,1,0:T(8,128)(2,1)S(1)}, u32[]{:S(2)}, u32[]{:S(2)}) collective-permute-start(bf16[1,2,264,128]{3,2,1,0:T(8,128)(2,1)S(1)} %get-tuple-element.28), channel_id=1, source_target_pairs={{0,4},{4,0},{1,5},{5,1},{2,6},{6,2},{3,7},{7,3},{8,12},{12,8},{9,1... | collective-permute-start | bytes 405512 | tf_op jit(solution)/shard_map/ppermute | solution.py:373
  14.1 5.5 %collective-permute-start.4 = (bf16[2,264,128]{2,1,0:T(8,128)(2,1)S(1)}, bf16[2,264,128]{2,1,0:T(8,128)(2,1)S(1)}, u32[]{:S(2)}, u32[]{:S(2)}) collective-permute-start(bf16[2,264,128]{2,1,0:T(8,128)(2,1)S(1)} %shard_map.90), channel_id=1, source_target_pairs={{0,1},{1,2},{2,3},{3,0},{4,5},{5,6},{6,7},{7,4},{8,9},{9,10},{10,1... | collective-permute-start | bytes 405512 | tf_op jit(solution)/shard_map/ppermute | solution.py:378
  14.2 5.3 %collective-permute-start.7 = (bf16[2,264,128]{2,1,0:T(8,128)(2,1)S(1)}, bf16[2,264,128]{2,1,0:T(8,128)(2,1)S(1)}, u32[]{:S(2)}, u32[]{:S(2)}) collective-permute-start(bf16[2,264,128]{2,1,0:T(8,128)(2,1)S(1)} %shard_map.91), channel_id=1, source_target_pairs={{0,3},{1,0},{2,1},{3,2},{4,7},{5,4},{6,5},{7,6},{8,11},{9,8},{10,9... | collective-permute-start | bytes 405512 | tf_op jit(solution)/shard_map/ppermute | solution.py:378
